TPU v7x, 128 devices: a whole 4x4x4 slice. The times are simulated.
128 devices in a mesh: seq: 32 (over z, y, core), head: 4 (over x).
Axes of the slice: x: 4, y: 4, z: 4, core: 2. Of those that a mesh axis runs over, the one named last changes fastest.
Arguments:
- queries: bfloat16 [2048, 32, 128], P('seq', 'head'), may hold values from -256 to 256
- keys: bfloat16 [65536, 16, 128], P('seq', 'head'), may hold values from -5 to 5
- values: bfloat16 [65536, 16, 128], P('seq', 'head'), may hold values from -6 to 6
- kv_len: int32 [32], P('seq'), may hold values from 1024 to 2048, as said below
- causal_offset: int32 [1], replicated, may hold values from 61440 to 63488
- out_weight: bfloat16 [4096, 4608], P('head'), may hold values from -0.09375 to 0.09375
Outputs:
- attn_out: float32 [2048, 4608], P('seq', 'head')
Inputs may be any that keep to these rules, and one draw needn't show every extreme that they name: `kv_len`: every shard is at least half full and some shard is completely full.
All inputs are finite; a program needn't handle non-finite values.
Results may differ from a plain program's by a relative error of at most 0.006.
Values may be sent and summed in bfloat16 or wider, within the bound.
A program may use at most 192 MiB of HBM per device.

v0:
```python
import jax
import jax.numpy as jnp
from jax import lax
from jax.sharding import PartitionSpec as P

score_scale = 1.0 / 12.0
floor_value = -1e30


def in_blocks(shard, dim, size):
    lengths = shard.shape
    parts = shard.reshape(*lengths[:dim], size, lengths[dim] // size, *lengths[dim + 1 :])
    return jnp.moveaxis(parts, dim, 0)


def sum_at_owner(shard, axis, dim):
    parts = in_blocks(shard, dim, lax.axis_size(axis))
    arrived = lax.all_to_all(parts, axis, split_axis=0, concat_axis=0, tiled=True)
    return arrived.sum(axis=0)


def shards(queries, keys, values, kv_len, causal_offset, out_weight):
    query_all = lax.all_gather(queries, "seq", axis=0, tiled=True)
    row_count, head_count, head_dim = query_all.shape
    kv_rows, group_count, _ = keys.shape
    pair_count = head_count // group_count
    query_groups = query_all.reshape(row_count, group_count, pair_count, head_dim)
    shard_idx = lax.axis_index("seq")
    length = kv_len[0]
    query_pos = causal_offset[0] + jnp.arange(row_count, dtype=jnp.int32)
    block_len = min(512, kv_rows)
    block_count = kv_rows // block_len

    def step(carry, block_idx):
        run_max, denom, numer = carry
        start = block_idx * block_len
        key_block = lax.dynamic_slice_in_dim(keys, start, block_len, 0)
        value_block = lax.dynamic_slice_in_dim(values, start, block_len, 0)
        scores = (
            jnp.einsum(
                "qgrd,kgd->qgrk", query_groups, key_block, preferred_element_type=jnp.float32
            )
            * score_scale
        )
        slot_idx = start + jnp.arange(block_len, dtype=jnp.int32)
        key_pos = shard_idx * kv_rows + slot_idx
        valid = (slot_idx < length)[None, :] & (key_pos[None, :] <= query_pos[:, None])
        valid = valid[:, None, None, :]
        new_max = jnp.maximum(run_max, jnp.max(jnp.where(valid, scores, floor_value), axis=-1))
        factor = jnp.exp(run_max - new_max)
        weights = jnp.where(valid, jnp.exp(scores - new_max[..., None]), 0.0)
        denom = denom * factor + jnp.sum(weights, axis=-1)
        numer = numer * factor[..., None] + jnp.einsum(
            "qgrk,kgd->qgrd",
            weights.astype(jnp.bfloat16),
            value_block,
            preferred_element_type=jnp.float32,
        )
        return ((new_max, denom, numer), None)

    init = (
        jnp.full((row_count, group_count, pair_count), floor_value, jnp.float32),
        jnp.zeros((row_count, group_count, pair_count), jnp.float32),
        jnp.zeros((row_count, group_count, pair_count, head_dim), jnp.float32),
    )
    (run_max, denom, numer), _ = lax.scan(step, init, jnp.arange(block_count, dtype=jnp.int32))
    numer_in, denom_in, max_in = (
        lax.all_to_all(numer[None], "seq", split_axis=1, concat_axis=0, tiled=True),
        lax.all_to_all(denom[None], "seq", split_axis=1, concat_axis=0, tiled=True),
        lax.all_to_all(run_max[None], "seq", split_axis=1, concat_axis=0, tiled=True),
    )
    global_max = jnp.max(max_in, axis=0)
    rescale = jnp.exp(max_in - global_max[None])
    owned_numer = jnp.sum(numer_in * rescale[..., None], axis=0)
    owned_denom = jnp.sum(denom_in * rescale, axis=0)
    owned_rows = owned_numer.shape[0]
    attended = (
        (owned_numer / owned_denom[..., None])
        .astype(jnp.bfloat16)
        .reshape(owned_rows, head_count * head_dim)
    )
    projected = jnp.dot(attended, out_weight, preferred_element_type=jnp.float32)
    return sum_at_owner(projected, "head", 1)


def solution(mesh):
    placed = (
        P("seq", "head", None),
        P("seq", "head", None),
        P("seq", "head", None),
        P("seq"),
        P(),
        P("head", None),
    )
    return jax.shard_map(
        shards, mesh=mesh, in_specs=placed, out_specs=P("seq", "head"), check_vma=False
    )
```

profile of v0, /device:TPU:1, one launch (start us, length us, event | category | flops | bytes accessed | tf_op | source)
XLA Modules:
  0.0 471.7 jit_solution(13979935339578852358)
XLA Ops:
  7.3 52.1 %all-gather.2.cloned.1.call-done = bf16[2048,8,128]{2,1,0:T(8,128)(2,1)} async-done(((bf16[64,8,128]{2,1,0:T(8,128)(2,1)}), bf16[2048,8,128]{2,1,0:T(8,128)(2,1)}) %all-gather.2.cloned.1.call-update) | async-done | bytes 4194320 | tf_op jit(solution)/shard_map/all_gather | solution.py:23
  64.1 222.1 %while.17 = (s32[]{:T(128)}, f32[2048,4,2]{0,2,1:T(2,128)S(1)}, f32[2048,4,2]{0,2,1:T(2,128)S(1)}, f32[2048,4,2,128]{0,3,2,1:T(8,128)}, s32[4]{0:T(128)S(1)}, /*...) while((s32[]{:T(128)}, f32[2048,4,2]{0,2,1:T(2,128)S(1)}, ...), condition=%wide.region_3.4_spmd.clone, body=%wide.region_0.3_spmd.clone.sunk | while | flops 4395716608 | bytes 131093736 | solution.py:66
  69.1 16.2 %fusion.37 = (f32[2048,4,2]{0,2,1:T(2,128)S(1)}, f32[4,512,2048,2]{2,1,3,0:T(8,128)}) fusion(pred[2048,512]{0,1:T(8,128)(4,1)S(1)} %compare_and_fusion.2, bf16[2048,4,2,128]{3,0,2,1:T(8,128)(2,1)} %get-tuple-element.378, bf16[512,4,128]{2,1,0:T(4,128)(2,1)S(1)} %get-tuple-element.334), kind=kOutput, calls=%fused_computation.3.clone.1 | convolution fusion | flops 2172633088 | bytes 39387136 | tf_op jit(solution)/shard_map/while/body/eval_jaxpr/qgrd,kgd->qgrk/dot_general | solution.py:40
  85.4 14.3 %fusion.39 = f32[2048,4,2]{0,2,1:T(2,128)S(1)} fusion(f32[4,512,2048,2]{2,1,3,0:T(8,128)} %get-tuple-element.336, f32[2048,4,2]{0,2,1:T(2,128)S(1)} %fusion.38, pred[2048,512]{0,1:T(8,128)(4,1)S(1)} %compare_and_fusion.2), kind=kLoop, calls=%fused_computation.7.clone.1 | loop fusion | flops 33538048 | bytes 34734080 | tf_op jit(solution)/shard_map/while/body/eval_jaxpr/reduce_sum | solution.py:52
  100.1 18.2 %bitcast_add_fusion.2 = f32[2048,4,2,128]{0,3,2,1:T(8,128)} fusion(f32[2048,4,2,128]{0,3,2,1:T(8,128)} %get-tuple-element.358, f32[4,512,2048,2]{2,1,3,0:T(8,128)} %get-tuple-element.336, f32[2048,4,2]{0,2,1:T(2,128)S(1)} %fusion.38, pred[2048,512]{0,1:T(8,128)(4,1)S(1)} %compare_and_fusion.2, f32[2048,4,2]{0,2,1:T(2,128)S(1)} %get-tuple-element.338, ...), kind=kOutput, calls=%fused_computation.10.clone.1 | convolution fusion | flops 2187329536 | bytes 52035584 | tf_op jit(solution)/shard_map/while/body/eval_jaxpr/qgrk,kgd->qgrd/dot_general | solution.py:53
  123.3 16.2 %fusion.37 = (f32[2048,4,2]{0,2,1:T(2,128)S(1)}, f32[4,512,2048,2]{2,1,3,0:T(8,128)}) fusion(pred[2048,512]{0,1:T(8,128)(4,1)S(1)} %compare_and_fusion.2, bf16[2048,4,2,128]{3,0,2,1:T(8,128)(2,1)} %get-tuple-element.378, bf16[512,4,128]{2,1,0:T(4,128)(2,1)S(1)} %get-tuple-element.334), kind=kOutput, calls=%fused_computation.3.clone.1 | convolution fusion | flops 2172633088 | bytes 39387136 | tf_op jit(solution)/shard_map/while/body/eval_jaxpr/qgrd,kgd->qgrk/dot_general | solution.py:40
  139.6 14.3 %fusion.39 = f32[2048,4,2]{0,2,1:T(2,128)S(1)} fusion(f32[4,512,2048,2]{2,1,3,0:T(8,128)} %get-tuple-element.336, f32[2048,4,2]{0,2,1:T(2,128)S(1)} %fusion.38, pred[2048,512]{0,1:T(8,128)(4,1)S(1)} %compare_and_fusion.2), kind=kLoop, calls=%fused_computation.7.clone.1 | loop fusion | flops 33538048 | bytes 34734080 | tf_op jit(solution)/shard_map/while/body/eval_jaxpr/reduce_sum | solution.py:52
  154.3 19.9 %bitcast_add_fusion.2 = f32[2048,4,2,128]{0,3,2,1:T(8,128)} fusion(f32[2048,4,2,128]{0,3,2,1:T(8,128)} %get-tuple-element.358, f32[4,512,2048,2]{2,1,3,0:T(8,128)} %get-tuple-element.336, f32[2048,4,2]{0,2,1:T(2,128)S(1)} %fusion.38, pred[2048,512]{0,1:T(8,128)(4,1)S(1)} %compare_and_fusion.2, f32[2048,4,2]{0,2,1:T(2,128)S(1)} %get-tuple-element.338, ...), kind=kOutput, calls=%fused_computation.10.clone.1 | convolution fusion | flops 2187329536 | bytes 52035584 | tf_op jit(solution)/shard_map/while/body/eval_jaxpr/qgrk,kgd->qgrd/dot_general | solution.py:53
  179.3 16.2 %fusion.37 = (f32[2048,4,2]{0,2,1:T(2,128)S(1)}, f32[4,512,2048,2]{2,1,3,0:T(8,128)}) fusion(pred[2048,512]{0,1:T(8,128)(4,1)S(1)} %compare_and_fusion.2, bf16[2048,4,2,128]{3,0,2,1:T(8,128)(2,1)} %get-tuple-element.378, bf16[512,4,128]{2,1,0:T(4,128)(2,1)S(1)} %get-tuple-element.334), kind=kOutput, calls=%fused_computation.3.clone.1 | convolution fusion | flops 2172633088 | bytes 39387136 | tf_op jit(solution)/shard_map/while/body/eval_jaxpr/qgrd,kgd->qgrk/dot_general | solution.py:40
  195.6 14.3 %fusion.39 = f32[2048,4,2]{0,2,1:T(2,128)S(1)} fusion(f32[4,512,2048,2]{2,1,3,0:T(8,128)} %get-tuple-element.336, f32[2048,4,2]{0,2,1:T(2,128)S(1)} %fusion.38, pred[2048,512]{0,1:T(8,128)(4,1)S(1)} %compare_and_fusion.2), kind=kLoop, calls=%fused_computation.7.clone.1 | loop fusion | flops 33538048 | bytes 34734080 | tf_op jit(solution)/shard_map/while/body/eval_jaxpr/reduce_sum | solution.py:52
  210.3 19.9 %bitcast_add_fusion.2 = f32[2048,4,2,128]{0,3,2,1:T(8,128)} fusion(f32[2048,4,2,128]{0,3,2,1:T(8,128)} %get-tuple-element.358, f32[4,512,2048,2]{2,1,3,0:T(8,128)} %get-tuple-element.336, f32[2048,4,2]{0,2,1:T(2,128)S(1)} %fusion.38, pred[2048,512]{0,1:T(8,128)(4,1)S(1)} %compare_and_fusion.2, f32[2048,4,2]{0,2,1:T(2,128)S(1)} %get-tuple-element.338, ...), kind=kOutput, calls=%fused_computation.10.clone.1 | convolution fusion | flops 2187329536 | bytes 52035584 | tf_op jit(solution)/shard_map/while/body/eval_jaxpr/qgrk,kgd->qgrd/dot_general | solution.py:53
  235.3 16.2 %fusion.37 = (f32[2048,4,2]{0,2,1:T(2,128)S(1)}, f32[4,512,2048,2]{2,1,3,0:T(8,128)}) fusion(pred[2048,512]{0,1:T(8,128)(4,1)S(1)} %compare_and_fusion.2, bf16[2048,4,2,128]{3,0,2,1:T(8,128)(2,1)} %get-tuple-element.378, bf16[512,4,128]{2,1,0:T(4,128)(2,1)S(1)} %get-tuple-element.334), kind=kOutput, calls=%fused_computation.3.clone.1 | convolution fusion | flops 2172633088 | bytes 39387136 | tf_op jit(solution)/shard_map/while/body/eval_jaxpr/qgrd,kgd->qgrk/dot_general | solution.py:40
  251.5 14.3 %fusion.39 = f32[2048,4,2]{0,2,1:T(2,128)S(1)} fusion(f32[4,512,2048,2]{2,1,3,0:T(8,128)} %get-tuple-element.336, f32[2048,4,2]{0,2,1:T(2,128)S(1)} %fusion.38, pred[2048,512]{0,1:T(8,128)(4,1)S(1)} %compare_and_fusion.2), kind=kLoop, calls=%fused_computation.7.clone.1 | loop fusion | flops 33538048 | bytes 34734080 | tf_op jit(solution)/shard_map/while/body/eval_jaxpr/reduce_sum | solution.py:52
  266.3 19.9 %bitcast_add_fusion.2 = f32[2048,4,2,128]{0,3,2,1:T(8,128)} fusion(f32[2048,4,2,128]{0,3,2,1:T(8,128)} %get-tuple-element.358, f32[4,512,2048,2]{2,1,3,0:T(8,128)} %get-tuple-element.336, f32[2048,4,2]{0,2,1:T(2,128)S(1)} %fusion.38, pred[2048,512]{0,1:T(8,128)(4,1)S(1)} %compare_and_fusion.2, f32[2048,4,2]{0,2,1:T(2,128)S(1)} %get-tuple-element.338, ...), kind=kOutput, calls=%fused_computation.10.clone.1 | convolution fusion | flops 2187329536 | bytes 52035584 | tf_op jit(solution)/shard_map/while/body/eval_jaxpr/qgrk,kgd->qgrd/dot_general | solution.py:53
  288.8 4.8 %reshape.95 = f32[32,1,512]{2,1,0:T(1,128)} reshape(f32[2048,1,2,4]{3,2,1,0:T(2,128)} %bitcast_bitcast_fusion.1) | data formatting | bytes 131072
  293.6 5.5 %all-to-all-start.1 = ((f32[32,1,512]{2,1,0:T(1,128)}), f32[32,1,512]{2,1,0:T(1,128)S(1)}, u32[]{:S(2)}, u32[]{:S(2)}) async-start(f32[32,1,512]{2,1,0:T(1,128)} %reshape.95), calls=%async_computation.1 | async-start | bytes 131072 | tf_op jit(solution)/shard_map/all_to_all | solution.py:70
  306.5 7.4 %all-to-all-start.2 = ((f32[32,1,512]{2,1,0:T(1,128)}), f32[32,1,512]{2,1,0:T(1,128)S(1)}, u32[]{:S(2)}, u32[]{:S(2)}) async-start(f32[32,1,512]{2,1,0:T(1,128)} %reshape.97), calls=%async_computation.2 | async-start | bytes 131072 | tf_op jit(solution)/shard_map/all_to_all | solution.py:69
  313.9 13.2 %copy.45 = f32[2048,4,2,128]{3,2,1,0:T(2,128)} copy(f32[2048,4,2,128]{0,3,2,1:T(8,128)} %get-tuple-element.134) | data formatting | bytes 16777216 | tf_op jit(solution)/shard_map/while | solution.py:66
  327.0 7.4 %all-to-all-start = ((f32[1,2048,4,2,128]{4,3,2,0,1:T(2,128)}), f32[1,2048,4,2,128]{4,3,2,0,1:T(2,128)}, u32[]{:S(2)}, u32[]{:S(2)}) async-start(f32[1,2048,4,2,128]{4,3,2,0,1:T(2,128)} %bitcast.72), calls=%async_computation | async-start | bytes 16777216 | tf_op jit(solution)/shard_map/all_to_all | solution.py:68
  334.5 12.7 %copy.58 = bf16[4608,1024]{1,0:T(8,128)(2,1)} copy(bf16[4608,1024]{0,1:T(8,128)(2,1)} %bitcast.76) | data formatting | bytes 18874368 | tf_op jit(solution)/shard_map/dot_general | solution.py:82
  359.1 76.0 %all-to-all-done = f32[1,2048,4,2,128]{4,3,2,0,1:T(2,128)} async-done(((f32[1,2048,4,2,128]{4,3,2,0,1:T(2,128)}), f32[1,2048,4,2,128]{4,3,2,0,1:T(2,128)}, u32[]{:S(2)}, u32[]{:S(2)}) %all-to-all-start) | async-done | bytes 8388640 | tf_op jit(solution)/shard_map/all_to_all | solution.py:68
  435.2 5.0 %copy.46 = f32[1,2048,4,2,128]{4,1,3,2,0:T(8,128)S(1)} copy(f32[1,2048,4,2,128]{4,3,2,0,1:T(2,128)} %all-to-all-done) | data formatting | bytes 16777216 | tf_op jit(solution)/shard_map/all_to_all | solution.py:68
  443.1 6.7 %convolution_bitcast_fusion = f32[4,64,1152]{2,1,0:T(8,128)S(1)} fusion(bf16[64,1024,1]{1,0,2:T(8,128)(2,1)S(1)} %reshape.93, bf16[4,1152,1024]{2,1,0:T(8,128)(2,1)} %bitcast.71), kind=kOutput, calls=%fused_computation.30 | convolution fusion | flops 603979776 | bytes 10747904 | tf_op jit(solution)/shard_map/dot_general | solution.py:82
  449.8 14.3 %all_to_all.41 = f32[4,64,1152]{2,1,0:T(8,128)S(1)} all-to-all(f32[4,64,1152]{2,1,0:T(8,128)S(1)} %convolution_bitcast_fusion), channel_id=1, replica_groups=mesh['seq'=32,'head'=4] {'head'}, dimensions={0} | all-to-all | bytes 2359296 | tf_op jit(solution)/shard_map/all_to_all | solution.py:18
  (69 shorter events, 50.0 us)
Async XLA Ops:
  6.5 52.9 %all-gather.2.cloned.1.call-start = ((), (), s32[]{:S(2)}) async-start(), calls=%async_computation.4 | async-start | bytes 4325376 | tf_op jit(solution)/shard_map/all_gather | solution.py:23
  293.6 12.9 %all-to-all-start.1 = ((f32[32,1,512]{2,1,0:T(1,128)}), f32[32,1,512]{2,1,0:T(1,128)S(1)}, u32[]{:S(2)}, u32[]{:S(2)}) async-start(f32[32,1,512]{2,1,0:T(1,128)} %reshape.95), calls=%async_computation.1 | async-start | bytes 131072 | tf_op jit(solution)/shard_map/all_to_all | solution.py:70
  306.5 20.6 %all-to-all-start.2 = ((f32[32,1,512]{2,1,0:T(1,128)}), f32[32,1,512]{2,1,0:T(1,128)S(1)}, u32[]{:S(2)}, u32[]{:S(2)}) async-start(f32[32,1,512]{2,1,0:T(1,128)} %reshape.97), calls=%async_computation.2 | async-start | bytes 131072 | tf_op jit(solution)/shard_map/all_to_all | solution.py:69
  327.0 108.2 %all-to-all-start = ((f32[1,2048,4,2,128]{4,3,2,0,1:T(2,128)}), f32[1,2048,4,2,128]{4,3,2,0,1:T(2,128)}, u32[]{:S(2)}, u32[]{:S(2)}) async-start(f32[1,2048,4,2,128]{4,3,2,0,1:T(2,128)} %bitcast.72), calls=%async_computation | async-start | bytes 16777216 | tf_op jit(solution)/shard_map/all_to_all | solution.py:68
Sparse Core Ops, SparseCore 0:
  9.6 49.7 all-gather.1
where the time goes:
time: 479 us; the launch traced here: 472 us
  matrix products  149 us (31%)
  waiting for transfers between devices  129 us (27%)
  other arithmetic  72.3 us (15%)
  local copies, waits for them, and re-layouts  69.8 us (15%)
  starting transfers between devices  20.3 us (4%)
  blocking collectives  14.3 us (3%)
  between operations  13.6 us (3%)
    dot_general x4, matrix products, step(): jnp.einsum('qgrk,kgd->qgrd', weights.astype(jnp.bfloat16), value_block, p...  78 us
    all_to_all x1, waiting for transfers between devices, shards(): lax.all_to_all(numer[None], 'seq', split_axis=1, concat_axis=0, tiled=True)  76 us
    dot_general x4, matrix products, step(): jnp.einsum('qgrd,kgd->qgrk', query_groups, key_block, preferred_element_t...  64.8 us
    reduce_sum x4, other arithmetic, step(): denom = denom * factor + jnp.sum(weights, axis=-1)  57.1 us
    all_gather x1, waiting for transfers between devices, shards(): query_all = lax.all_gather(queries, 'seq', axis=0, tiled=True)  52.1 us
    unnamed x7, local copies, waits for them, and re-layouts  23.6 us
    while x3, local copies, waits for them, and re-layouts, shards(): lax.scan(step, init, jnp.arange(block_count, dtype=jnp.int32))  15.4 us
    all_to_all x1, blocking collectives, sum_at_owner(): lax.all_to_all(parts, axis, split_axis=0, concat_axis=0, tiled=True)  14.3 us
  transfers between devices with their start and end apart: 4, of which 2 were waited for; matrix products, arithmetic and copies ran while one was open for 10% of the time, Pallas kernels for 0%

commit v1 on v0

v1 whole, which is shorter than its diff:
```python
import functools
import math

import jax
import jax.numpy as jnp
from jax import lax
from jax.experimental import pallas as pl
from jax.experimental.pallas import tpu as pltpu
from jax.sharding import PartitionSpec as P

bf16 = jnp.bfloat16
f32 = jnp.float32
MESH = pl.DeviceIdType.MESH
score_scale = math.log2(math.e) / 12.0
masked_score = -1e30
HD = 128
CHIPS = 16
ROWS = 64
SLOTS = 2048
VROWS = 144
CH = 256
NCH = 2 * SLOTS // CH
VMEM_LIMIT = 60 * 2**20


def place():
    seq = lax.axis_index("seq")
    head = lax.axis_index("head")
    chip = seq // 2
    return seq, head, chip // 4, chip % 4, seq % 2


def dev(z, y, core, head):
    return ((z * 4 + y) * 2 + core, head)


def enter(peers):
    barrier = pltpu.get_barrier_semaphore()
    for peer in peers:
        pl.semaphore_signal(barrier, inc=1, device_id=peer, device_id_type=MESH)
    pl.semaphore_wait(barrier, len(peers))


def remote(src, dst, send_sem, recv_sem, device):
    return pltpu.make_async_remote_copy(
        src_ref=src,
        dst_ref=dst,
        send_sem=send_sem,
        recv_sem=recv_sem,
        device_id=device,
        device_id_type=MESH,
    )


def gather_kernel(
    len_ref, q_ref, k_ref, v_ref, qg, kg, vg,
    wide, qs, ks, vs, local_sem, psend, precv, ysend, yrecv, zsend, zrecv, fsend, frecv,
):
    seq, head, z, y, c = place()
    p = 1 - c
    partner = dev(z, y, p, head)
    peers = [partner]
    for d in (1, 2, 3):
        for tc in (0, 1):
            peers.append(dev(z, (y + d) % 4, tc, head))
            peers.append(dev((z + d) % 4, y, tc, head))

    wide[0:512, :] = q_ref[...].astype(f32)
    for h in range(8):
        qs[h] = wide[pl.ds(h, ROWS, stride=8), :].astype(bf16)
    enter(peers)

    first = []
    own = (z * 4 + y) * 2 + c
    copy = remote(qs.at[pl.ds(4 * p, 4)], qg.at[z, y, c], psend.at[0], precv.at[0], partner)
    copy.start()
    first.append(copy)
    for d in (1, 2, 3):
        for tc in (0, 1):
            copy = remote(
                qs.at[pl.ds(4 * tc, 2)], qg.at[z, y, c, pl.ds(0, 2)],
                ysend.at[d - 1, tc], yrecv.at[d - 1, c], dev(z, (y + d) % 4, tc, head),
            )
            copy.start()
            first.append(copy)
            copy = remote(
                qs.at[pl.ds(4 * tc + 2, 2)], qg.at[z, y, c, pl.ds(2, 2)],
                zsend.at[d - 1, tc], zrecv.at[d - 1, c], dev((z + d) % 4, y, tc, head),
            )
            copy.start()
            first.append(copy)
    mine_q = pltpu.make_async_copy(qs.at[pl.ds(4 * c, 4)], qg.at[z, y, c], local_sem.at[0])
    mine_q.start()

    length = len_ref[0]
    rows = 256
    k0 = k_ref[0:8, :].astype(f32)

    def relayout(b, _):
        slot = lax.broadcasted_iota(jnp.int32, (rows, HD), 0) + b * rows
        filled = slot < length
        wide[...] = k_ref[pl.ds(pl.multiple_of(b * rows * 4, rows * 4), rows * 4), :].astype(f32)
        for h in range(4):
            part = wide[pl.ds(h, rows, stride=4), :]
            part = jnp.where(filled, part, k0[h : h + 1, :])
            ks[h, pl.ds(pl.multiple_of(b * rows, rows), rows), :] = part.astype(bf16)
        wide[...] = v_ref[pl.ds(pl.multiple_of(b * rows * 4, rows * 4), rows * 4), :].astype(f32)
        col = lax.broadcasted_iota(jnp.int32, (16, rows), 1) + b * rows
        row = lax.broadcasted_iota(jnp.int32, (16, rows), 0)
        ones = jnp.where((col < length) & (row == 0), 1.0, 0.0).astype(bf16)
        for h in range(4):
            part = wide[pl.ds(h, rows, stride=4), :]
            part = jnp.where(filled, part, 0.0)
            cols = pl.ds(pl.multiple_of(b * rows, rows), rows)
            vs[h, 0:HD, cols] = part.T.astype(bf16)
            vs[h, HD:VROWS, cols] = ones
        return 0

    lax.fori_loop(0, SLOTS // rows, relayout, 0)
    send_k = remote(ks.at[pl.ds(2 * p, 2)], kg.at[c], psend.at[1], precv.at[1], partner)
    send_v = remote(vs.at[pl.ds(2 * p, 2)], vg.at[c], psend.at[2], precv.at[2], partner)
    send_k.start()
    send_v.start()
    mine_k = pltpu.make_async_copy(ks.at[pl.ds(2 * c, 2)], kg.at[c], local_sem.at[1])
    mine_v = pltpu.make_async_copy(vs.at[pl.ds(2 * c, 2)], vg.at[c], local_sem.at[2])
    mine_k.start()
    mine_v.start()

    mine_q.wait()
    for copy in first:
        copy.wait_send()
    first[0].wait_recv()
    for d in (1, 2, 3):
        for sc in (0, 1):
            remote(
                qs.at[pl.ds(0, 2)], qg.at[z, (y + 4 - d) % 4, sc, pl.ds(0, 2)],
                ysend.at[d - 1, sc], yrecv.at[d - 1, sc], partner,
            ).wait_recv()
            remote(
                qs.at[pl.ds(0, 2)], qg.at[(z + 4 - d) % 4, y, sc, pl.ds(2, 2)],
                zsend.at[d - 1, sc], zrecv.at[d - 1, sc], partner,
            ).wait_recv()

    second = []
    for d in (1, 2, 3):
        src = qg.at[z, :, :, pl.ds(0, 2)]
        copy = remote(src, src, fsend.at[0, d - 1], frecv.at[0, d - 1], dev((z + d) % 4, y, c, head))
        copy.start()
        second.append(copy)
        src = qg.at[:, y, :, pl.ds(2, 2)]
        copy = remote(src, src, fsend.at[1, d - 1], frecv.at[1, d - 1], dev(z, (y + d) % 4, c, head))
        copy.start()
        second.append(copy)
    for copy in second:
        copy.wait_send()
    for d in (1, 2, 3):
        src = qg.at[(z + 4 - d) % 4, :, :, pl.ds(0, 2)]
        remote(src, src, fsend.at[0, d - 1], frecv.at[0, d - 1], partner).wait_recv()
        src = qg.at[:, (y + 4 - d) % 4, :, pl.ds(2, 2)]
        remote(src, src, fsend.at[1, d - 1], frecv.at[1, d - 1], partner).wait_recv()
    send_k.wait()
    send_v.wait()
    mine_k.wait()
    mine_v.wait()


def gather(length, q, k, v):
    dma = pltpu.SemaphoreType.DMA
    vmem = pl.BlockSpec(memory_space=pltpu.VMEM)
    hbm = pl.BlockSpec(memory_space=pl.ANY)
    return pl.pallas_call(
        gather_kernel,
        out_shape=(
            jax.ShapeDtypeStruct((4, 4, 2, 4, ROWS, HD), bf16),
            jax.ShapeDtypeStruct((2, 2, SLOTS, HD), bf16),
            jax.ShapeDtypeStruct((2, 2, VROWS, SLOTS), bf16),
        ),
        in_specs=[pl.BlockSpec(memory_space=pltpu.SMEM), vmem, vmem, vmem],
        out_specs=(hbm, hbm, hbm),
        scratch_shapes=[
            pltpu.VMEM((1024, HD), f32),
            pltpu.VMEM((8, ROWS, HD), bf16),
            pltpu.VMEM((4, SLOTS, HD), bf16),
            pltpu.VMEM((4, VROWS, SLOTS), bf16),
            dma((3,)),
            dma((3,)),
            dma((3,)),
            dma((3, 2)),
            dma((3, 2)),
            dma((3, 2)),
            dma((3, 2)),
            dma((2, 3)),
            dma((2, 3)),
        ],
        compiler_params=pltpu.CompilerParams(
            collective_id=0, has_side_effects=True, vmem_limit_bytes=VMEM_LIMIT
        ),
        name="gather",
    )(length, q, k, v)


def attention_kernel(off_ref, q_ref, k_ref, vt_ref, o_ref, m_ref, s0, s1):
    seq = lax.axis_index("seq")
    last_chip = seq // 2 == CHIPS - 1
    first_key = (SLOTS * 2) * (CHIPS - 1)
    offset = off_ref[0] - first_key

    def queries_of(tile):
        chip, group = tile // 2, tile % 2
        parts = [q_ref[chip // 4, chip % 4, c, group * 2 + h] for h in (0, 1) for c in (0, 1)]
        q = jnp.concatenate(parts, axis=0).astype(f32) * score_scale
        high = q.astype(bf16)
        low = (q - high.astype(f32)).astype(bf16)
        return jnp.concatenate([high, low], axis=1)

    def tiles(tn, sn, tc, sc, m_now, causal):
        m = jnp.full((8, 256), masked_score, f32)
        if tn is not None:
            qq = queries_of(tn)
            if causal:
                lane = lax.broadcasted_iota(jnp.int32, (8, 256), 1) % HD
                limit = offset + (tn // 2) * HD + lane - lax.broadcasted_iota(jnp.int32, (8, 256), 0)
        acc = jnp.zeros((VROWS, 256), f32)
        for c in range(NCH):
            shard, start = c // 8, (c % 8) * CH
            if tn is not None:
                k = k_ref[shard, tn % 2, pl.ds(start, CH), :]
                kk = jnp.concatenate([k, k], axis=1)
                s = lax.dot_general(kk, qq, (((1,), (1,)), ((), ())), preferred_element_type=f32)
                s = s.reshape(CH // 8, 8, 256)
                if causal:
                    s = jnp.stack(
                        [
                            jnp.where(limit >= c * CH + 8 * i, s[i], masked_score)
                            for i in range(CH // 8)
                        ]
                    )
                sn[pl.ds(c * CH, CH), :] = s.reshape(CH, 256)
                m = jnp.maximum(m, jnp.max(s, axis=0))
            if tc is not None:
                s = sc[pl.ds(c * CH, CH), :].reshape(CH // 8, 8, 256)
                prob = jnp.exp2(s - m_now[None]).reshape(CH, 256).astype(bf16)
                vt = vt_ref[shard, tc % 2, :, pl.ds(start, CH)]
                acc = acc + jnp.dot(vt, prob, preferred_element_type=f32)
        if tc is not None:
            chip, group = tc // 2, tc % 2
            o_ref[chip // 4, chip % 4, group] = acc[:HD].astype(bf16)
            m_ref[chip // 4, chip % 4, group, 0:1, :] = m_now[0:1]
            m_ref[chip // 4, chip % 4, group, 1:2, :] = acc[HD : HD + 1]
        if tn is not None:
            return jnp.broadcast_to(jnp.max(m, axis=0, keepdims=True), (8, 256))

    def run(causal):
        m = tiles(0, s0, None, None, None, causal)

        def body(u, m):
            m = tiles(2 * u + 1, s1, 2 * u, s0, m, causal)
            return tiles(jnp.minimum(2 * u + 2, 31), s0, 2 * u + 1, s1, m, causal)

        lax.fori_loop(0, CHIPS, body, m)

    @pl.when(jnp.logical_not(last_chip))
    def _():
        run(False)

    @pl.when(last_chip)
    def _():
        run(True)


def attention(offset, q, k, vt):
    vmem = pl.BlockSpec(memory_space=pltpu.VMEM)
    return pl.pallas_call(
        attention_kernel,
        out_shape=(
            jax.ShapeDtypeStruct((4, 4, 2, HD, 256), bf16),
            jax.ShapeDtypeStruct((4, 4, 2, 2, 256), f32),
        ),
        in_specs=[pl.BlockSpec(memory_space=pltpu.SMEM), vmem, vmem, vmem],
        out_specs=(vmem, vmem),
        scratch_shapes=[pltpu.VMEM((2 * SLOTS, 256), f32), pltpu.VMEM((2 * SLOTS, 256), f32)],
        compiler_params=pltpu.CompilerParams(vmem_limit_bytes=VMEM_LIMIT),
        name="attention",
    )(offset, q, k, vt)


def merge(parts):
    top = parts[0][1]
    for _, m, _ in parts[1:]:
        top = jnp.maximum(top, m)
    numer, denom = None, None
    for o, m, l in parts:
        factor = jnp.exp2(m - top)
        o = o.astype(f32) * factor
        l = l * factor
        numer = o if numer is None else numer + o
        denom = l if denom is None else denom + l
    return numer, top, denom


def reduce_kernel(
    o_ref, m_ref, w_ref, out_ref,
    w, own1, ownm, in1, inm1, mid, midm, in2, inm2, att, half, part, inx,
    wsem, lsem, s1, r1, s1m, r1m, s2, r2, s2m, r2m, ps, pr, xs, xr,
):
    seq, head, z, y, c = place()
    p = 1 - c
    partner = dev(z, y, p, head)
    weights = pltpu.make_async_copy(w_ref, w, wsem)
    weights.start()
    peers = [partner]
    for d in (1, 2, 3):
        peers.append(dev(z, (y + d) % 4, c, head))
        peers.append(dev((z + d) % 4, y, c, head))
        peers.append((seq, (head + d) % 4))

    locals_ = [
        pltpu.make_async_copy(o_ref.at[z, :, 0], own1.at[0], lsem.at[0]),
        pltpu.make_async_copy(o_ref.at[:, y, 1], own1.at[1], lsem.at[1]),
        pltpu.make_async_copy(m_ref.at[z, :, 0], ownm.at[0], lsem.at[2]),
        pltpu.make_async_copy(m_ref.at[:, y, 1], ownm.at[1], lsem.at[3]),
    ]
    for copy in locals_:
        copy.start()
    enter(peers)

    first = []
    for d in (2, 1, 3):
        zt, yt = (z + d) % 4, (y + d) % 4
        for copy in (
            remote(m_ref.at[zt, :, 0], inm1.at[0, d - 1], s1m.at[0, d - 1], r1m.at[0, d - 1], dev(zt, y, c, head)),
            remote(m_ref.at[:, yt, 1], inm1.at[1, d - 1], s1m.at[1, d - 1], r1m.at[1, d - 1], dev(z, yt, c, head)),
            remote(o_ref.at[zt, :, 0], in1.at[0, d - 1], s1.at[0, d - 1], r1.at[0, d - 1], dev(zt, y, c, head)),
            remote(o_ref.at[:, yt, 1], in1.at[1, d - 1], s1.at[1, d - 1], r1.at[1, d - 1], dev(z, yt, c, head)),
        ):
            copy.start()
            first.append(copy)
    for copy in locals_:
        copy.wait()
    for copy in first:
        copy.wait()

    def sum_first(i, _):
        for g in (0, 1):
            parts = [(own1[g, i], ownm[g, i, 0:1, :], ownm[g, i, 1:2, :])]
            for d in range(3):
                parts.append((in1[g, d, i], inm1[g, d, i, 0:1, :], inm1[g, d, i, 1:2, :]))
            numer, top, denom = merge(parts)
            mid[g, i] = numer.astype(bf16)
            midm[g, i, 0:1, :] = top
            midm[g, i, 1:2, :] = denom
        return 0

    lax.fori_loop(0, 4, sum_first, 0)
    second = []
    for d in (2, 1, 3):
        zt, yt = (z + d) % 4, (y + d) % 4
        for copy in (
            remote(midm.at[0, yt], inm2.at[0, d - 1], s2m.at[0, d - 1], r2m.at[0, d - 1], dev(z, yt, c, head)),
            remote(midm.at[1, zt], inm2.at[1, d - 1], s2m.at[1, d - 1], r2m.at[1, d - 1], dev(zt, y, c, head)),
            remote(mid.at[0, yt], in2.at[0, d - 1], s2.at[0, d - 1], r2.at[0, d - 1], dev(z, yt, c, head)),
            remote(mid.at[1, zt], in2.at[1, d - 1], s2.at[1, d - 1], r2.at[1, d - 1], dev(zt, y, c, head)),
        ):
            copy.start()
            second.append(copy)
    for copy in second:
        copy.wait()
    for g in (0, 1):
        me = y if g == 0 else z
        parts = [(mid[g, me], midm[g, me, 0:1, :], midm[g, me, 1:2, :])]
        for d in range(3):
            parts.append((in2[g, d], inm2[g, d, 0:1, :], inm2[g, d, 1:2, :]))
        numer, _, denom = merge(parts)
        done = numer / denom
        for h in (0, 1):
            rows = done[:, h * HD : (h + 1) * HD].T.astype(bf16)
            cols = slice((g * 2 + h) * HD, (g * 2 + h + 1) * HD)
            half[0, :, cols] = rows[:ROWS]
            half[1, :, cols] = rows[ROWS:]

    swap = remote(half.at[p], att.at[c], ps, pr, partner)
    swap.start()
    weights.wait()
    swap.wait()
    lhs = jnp.concatenate(
        [
            jnp.where(c == 0, half[0], att[0]),
            jnp.where(c == 0, att[1], half[1]),
        ],
        axis=1,
    )
    cols = 1152
    sends = []
    for d in (2, 1, 3, 0):
        target = (head + d) % 4
        block = jnp.dot(
            lhs, w[:, pl.ds(pl.multiple_of(target * cols, HD), cols)], preferred_element_type=f32
        )
        if d:
            part[d - 1] = block.astype(bf16)
            copy = remote(part.at[d - 1], inx.at[d - 1], xs.at[d - 1], xr.at[d - 1], (seq, target))
            copy.start()
            sends.append(copy)
        else:
            total = block
    for copy in sends:
        copy.wait()
    out_ref[...] = total + (
        (inx[0].astype(f32) + inx[1].astype(f32)) + inx[2].astype(f32)
    )


def reduction(o, m, weight):
    dma = pltpu.SemaphoreType.DMA
    hbm = pl.BlockSpec(memory_space=pl.ANY)
    return pl.pallas_call(
        reduce_kernel,
        out_shape=jax.ShapeDtypeStruct((ROWS, 1152), f32),
        in_specs=[hbm, hbm, hbm],
        out_specs=pl.BlockSpec(memory_space=pltpu.VMEM),
        scratch_shapes=[
            pltpu.VMEM((1024, 4608), bf16),
            pltpu.VMEM((2, 4, HD, 256), bf16),
            pltpu.VMEM((2, 4, 2, 256), f32),
            pltpu.VMEM((2, 3, 4, HD, 256), bf16),
            pltpu.VMEM((2, 3, 4, 2, 256), f32),
            pltpu.VMEM((2, 4, HD, 256), bf16),
            pltpu.VMEM((2, 4, 2, 256), f32),
            pltpu.VMEM((2, 3, HD, 256), bf16),
            pltpu.VMEM((2, 3, 2, 256), f32),
            pltpu.VMEM((2, ROWS, 512), bf16),
            pltpu.VMEM((2, ROWS, 512), bf16),
            pltpu.VMEM((3, ROWS, 1152), bf16),
            pltpu.VMEM((3, ROWS, 1152), bf16),
            dma,
            dma((4,)),
            dma((2, 3)),
            dma((2, 3)),
            dma((2, 3)),
            dma((2, 3)),
            dma((2, 3)),
            dma((2, 3)),
            dma((2, 3)),
            dma((2, 3)),
            dma,
            dma,
            dma((3,)),
            dma((3,)),
        ],
        compiler_params=pltpu.CompilerParams(
            collective_id=1, has_side_effects=True, vmem_limit_bytes=VMEM_LIMIT
        ),
        name="reduction",
    )(o, m, weight)


def shards(queries, keys, values, kv_len, causal_offset, out_weight):
    q, k, vt = gather(
        kv_len,
        queries.reshape(ROWS * 8, HD),
        keys.reshape(SLOTS * 4, HD),
        values.reshape(SLOTS * 4, HD),
    )
    o, m = attention(causal_offset, q, k, vt)
    return reduction(o, m, out_weight)


def solution(mesh):
    placed = (
        P("seq", "head", None),
        P("seq", "head", None),
        P("seq", "head", None),
        P("seq"),
        P(),
        P("head", None),
    )
    return jax.shard_map(
        shards, mesh=mesh, in_specs=placed, out_specs=P("seq", "head"), check_vma=False
    )
```

time: 479 us -> 107 us (0.22); the launches traced: 472 us -> 107 us
  matrix products: 149 us -> 0 us
  waiting for transfers between devices: 129 us -> 0 us
  Pallas kernels: 0 us -> 104 us
  other arithmetic: 72.3 us -> 0 us
  local copies, waits for them, and re-layouts: 69.8 us -> 1.69 us
  starting transfers between devices: 20.3 us -> 0 us
  blocking collectives: 14.3 us -> 0 us
  between operations: 13.6 us -> 1.31 us
    dot_general x9 -> x0, matrix products: 149 us -> none  [the longest x4 78 us: step(): jnp.einsum('qgrk,kgd->qgrd', weights.astype(jnp.bfloat16), value_block, p...]
    pallas_call x0 -> x3, Pallas kernels: none -> 104 us  [the longest x1 38.8 us: attention(): pl.pallas_call(attention_kernel, out_shape=(jax.ShapeDtypeStruct((4, 4, 2...]
    all_to_all x3 -> x0, waiting for transfers between devices: 76.1 us -> none  [the longest x1 76 us: shards(): lax.all_to_all(numer[None], 'seq', split_axis=1, concat_axis=0, tiled=True)]
    reduce_sum x7 -> x0, other arithmetic: 60.5 us -> none  [the longest x4 57.1 us: step(): denom = denom * factor + jnp.sum(weights, axis=-1)]
    all_gather x1 -> x0, waiting for transfers between devices: 52.1 us -> none  [shards(): query_all = lax.all_gather(queries, 'seq', axis=0, tiled=True)]
    unnamed x7 -> x1, local copies, waits for them, and re-layouts: 23.6 us -> 1.69 us
    all_to_all x3 -> x0, starting transfers between devices: 20.3 us -> none  [the longest x1 7.44 us: shards(): lax.all_to_all(numer[None], 'seq', split_axis=1, concat_axis=0, tiled=True)]
    while x7 -> x0, local copies, waits for them, and re-layouts: 15.4 us -> none  [the longest x3 15.4 us: shards(): lax.scan(step, init, jnp.arange(block_count, dtype=jnp.int32))]
  transfers between devices with their start and end apart: 4 -> 0, of which waited for: 2 -> 0; matrix products, arithmetic and copies ran while one was open for 10% -> 0% of each run, Pallas kernels for 0% -> 0%
where the time goes in v1:
time: 107 us
  Pallas kernels  104 us (97%)
  local copies, waits for them, and re-layouts  1.69 us (2%)
  between operations  1.31 us (1%)
    pallas_call x1, Pallas kernels, attention(): pl.pallas_call(attention_kernel, out_shape=(jax.ShapeDtypeStruct((4, 4, 2...  38.8 us
    pallas_call x1, Pallas kernels, reduction(): pl.pallas_call(reduce_kernel, out_shape=jax.ShapeDtypeStruct((ROWS, 1152)...  37.2 us
    pallas_call x1, Pallas kernels, gather(): pl.pallas_call(gather_kernel, out_shape=(jax.ShapeDtypeStruct((4, 4, 2, 4...  28.3 us

profile of v1, /device:TPU:1, one launch (start us, length us, event | category | flops | bytes accessed | tf_op | source)
XLA Modules:
  0.0 107.3 jit_solution(11235494449840890164)
XLA Ops:
  1.3 28.3 %gather.1 = (bf16[4,4,2,4,64,128]{5,4,3,2,1,0:T(8,128)(2,1)}, bf16[2,2,2048,128]{3,2,1,0:T(8,128)(2,1)}, bf16[2,2,144,2048]{3,2,1,0:T(8,128)(2,1)}) custom-call(s32[1]{0:T(128)S(6)} %copy.8.len_ref, bf16[512,128]{1,0:T(8,128)(2,1)} %bitcast.5, bf16[8192,128]{1,0:T(8,128)(2,1)} %bitcast.3, bf16[8192,128]{1,0:T(8,128)(2,1)} %bitcast.4), custom_call_target="tpu_custom_call" | custom-call | tf_op jit(solution)/shard_map/gather/pallas_call | solution.py:171
  29.6 38.8 %attention.1 = (bf16[4,4,2,128,256]{4,3,2,1,0:T(8,128)(2,1)}, f32[4,4,2,2,256]{4,3,2,1,0:T(2,128)}) custom-call(s32[1]{0:T(128)S(6)} %copy.9.off_ref, bf16[4,4,2,4,64,128]{5,4,3,2,1,0:T(8,128)(2,1)} %get-tuple-element.10.q_ref, bf16[2,2,2048,128]{3,2,1,0:T(8,128)(2,1)} %get-tuple-element.11.k_ref, bf16[2,2,144,2048]{3,2,1,0:T(8,128)(2,1)} %get-tuple-element.12.vt_ref), custom_call_target="tpu_custom_call" | custom-call | tf_op jit(solution)/shard_map/attention/pallas_call | solution.py:273
  68.4 37.2 %reduction.1 = f32[64,1152]{1,0:T(8,128)} custom-call(bf16[4,4,2,128,256]{4,3,2,1,0:T(8,128)(2,1)} %get-tuple-element.13.o_ref, f32[4,4,2,2,256]{4,3,2,1,0:T(2,128)} %get-tuple-element.14.m_ref, bf16[1024,4608]{1,0:T(8,128)(2,1)} %w_ref.1), custom_call_target="tpu_custom_call" | custom-call | tf_op jit(solution)/shard_map/reduction/pallas_call | solution.py:416
  105.6 1.7 %copy.10 = f32[64,1152]{1,0:T(8,128)} copy(f32[64,1152]{1,0:T(8,128)} %reduction.1) | data formatting | bytes 589824

commit v2 on v0

v2 whole, which is shorter than its diff:
```python
import math

import jax
import jax.numpy as jnp
from jax import lax
from jax.experimental import pallas as pl
from jax.experimental.pallas import tpu as pltpu
from jax.sharding import PartitionSpec as P

bf16 = jnp.bfloat16
f32 = jnp.float32
MESH = pl.DeviceIdType.MESH
score_scale = math.log2(math.e) / 12.0
masked_score = -1e30
HD = 128
ROWS = 64
SLOTS = 2048
VROWS = 144
CH = 256
COLS = 1152
BLOCK = 256
BLOCKS = SLOTS // BLOCK


def remote(src, dst, send_sem, recv_sem, device):
    return pltpu.make_async_remote_copy(
        src_ref=src,
        dst_ref=dst,
        send_sem=send_sem,
        recv_sem=recv_sem,
        device_id=device,
        device_id_type=MESH,
    )


def merge(parts):
    top = parts[0][1]
    for _, m, _ in parts[1:]:
        top = jnp.maximum(top, m)
    numer, denom = None, None
    for o, m, l in parts:
        factor = jnp.exp2(m - top)
        o = o.astype(f32) * factor
        l = l * factor
        numer = o if numer is None else numer + o
        denom = l if denom is None else denom + l
    return numer, top, denom


def kernel(
    len_ref, off_ref, q_hbm, k_hbm, v_hbm, w_hbm, out_ref,
    q_raw, k_raw, v_raw, w, wide, qs, ks, vs, kp, vp, qg, s0, s1, tops,
    o_own, m_own, in1, inm1, mid, midm, in2, inm2, half, att, part, inx,
    lsem, kl, vl, psend, precv, ysend, yrecv, zsend, zrecv, fsend, frecv,
    ksend, krecv, vsend, vrecv, s1s, s1r, s1ms, s1mr, s2s, s2r, s2ms, s2mr, as_, ar, xs, xr,
):
    seq = lax.axis_index("seq")
    head = lax.axis_index("head")
    z, y, c = seq // 8, (seq // 2) % 4, seq % 2
    p = 1 - c

    def dev(zt, yt, core):
        return ((zt * 4 + yt) * 2 + core, head)

    def ahead(index, d):
        return lax.rem(index + d, 4)

    partner = dev(z, y, p)

    load_q = pltpu.make_async_copy(q_hbm, q_raw, lsem.at[0])
    load_w = pltpu.make_async_copy(w_hbm, w, lsem.at[1])

    def load_kv(b):
        rows = pl.ds(pl.multiple_of(b * BLOCK * 4, BLOCK * 4), BLOCK * 4)
        return (
            pltpu.make_async_copy(k_hbm.at[rows], k_raw.at[rows], kl.at[b]),
            pltpu.make_async_copy(v_hbm.at[rows], v_raw.at[rows], vl.at[b]),
        )

    load_q.start()
    for b in range(BLOCKS):
        for copy in load_kv(b):
            copy.start()
    load_w.start()

    peers = [partner]
    for d in (1, 2, 3):
        for core in (0, 1):
            peers.append(dev(z, ahead(y, d), core))
            peers.append(dev(ahead(z, d), y, core))
        peers.append((seq, ahead(head, d)))
    barrier = pltpu.get_barrier_semaphore()
    for peer in peers:
        pl.semaphore_signal(barrier, inc=1, device_id=peer, device_id_type=MESH)

    load_q.wait()
    wide[0 : ROWS * 8, :] = q_raw[...].astype(f32)
    for h in range(8):
        qs[h] = wide[pl.ds(h, ROWS, stride=8), :].astype(bf16)
    qg[z, y, c] = qs[pl.ds(4 * c, 4)]

    length = len_ref[0]

    def prepare(b, _):
        for copy in load_kv(b):
            copy.wait()
        k0 = k_raw[0:8, :].astype(f32)
        rows = pl.ds(pl.multiple_of(b * BLOCK * 4, BLOCK * 4), BLOCK * 4)
        slots = pl.ds(pl.multiple_of(b * BLOCK, BLOCK), BLOCK)
        filled = lax.broadcasted_iota(jnp.int32, (BLOCK, HD), 0) + b * BLOCK < length
        wide[...] = k_raw[rows, :].astype(f32)
        for h in range(4):
            one = wide[pl.ds(h, BLOCK, stride=4), :]
            ks[h, slots, :] = jnp.where(filled, one, k0[h : h + 1, :]).astype(bf16)
        wide[...] = v_raw[rows, :].astype(f32)
        col = lax.broadcasted_iota(jnp.int32, (VROWS - HD, BLOCK), 1) + b * BLOCK
        row = lax.broadcasted_iota(jnp.int32, (VROWS - HD, BLOCK), 0)
        ones = jnp.where((col < length) & (row == 0), 1.0, 0.0).astype(bf16)
        for h in range(4):
            one = wide[pl.ds(h, BLOCK, stride=4), :]
            vs[h, 0:HD, slots] = jnp.where(filled, one, 0.0).T.astype(bf16)
            vs[h, HD:VROWS, slots] = ones
        return 0

    def swap_kv(b):
        slots = pl.ds(pl.multiple_of(b * BLOCK, BLOCK), BLOCK)
        return (
            remote(ks.at[pl.ds(2 * p, 2), slots], kp.at[:, slots], ksend.at[b], krecv.at[b], partner),
            remote(
                vs.at[pl.ds(2 * p, 2), :, slots], vp.at[:, :, slots], vsend.at[b], vrecv.at[b], partner
            ),
        )

    lax.fori_loop(0, BLOCKS // 2, prepare, 0)
    pl.semaphore_wait(barrier, len(peers))

    first = [remote(qs.at[pl.ds(4 * p, 4)], qg.at[z, y, c], psend, precv, partner)]
    for d in (1, 3, 2):
        for core in (0, 1):
            first.append(
                remote(
                    qs.at[pl.ds(4 * core, 2)], qg.at[z, y, c, pl.ds(0, 2)],
                    ysend.at[d - 1, core], yrecv.at[d - 1, c], dev(z, ahead(y, d), core),
                )
            )
            first.append(
                remote(
                    qs.at[pl.ds(4 * core + 2, 2)], qg.at[z, y, c, pl.ds(2, 2)],
                    zsend.at[d - 1, core], zrecv.at[d - 1, c], dev(ahead(z, d), y, core),
                )
            )
    for copy in first:
        copy.start()

    def start_swap(b, _):
        for copy in swap_kv(b):
            copy.start()
        return 0

    lax.fori_loop(0, BLOCKS // 2, start_swap, 0)
    lax.fori_loop(BLOCKS // 2, BLOCKS, prepare, 0)
    lax.fori_loop(BLOCKS // 2, BLOCKS, start_swap, 0)

    last_chip = (z == 3) & (y == 3)
    offset = off_ref[0] - 30 * SLOTS

    def queries_of(zq, yq, group):
        parts = [qg[zq, yq, core, group * 2 + h] for h in (0, 1) for core in (0, 1)]
        q = jnp.concatenate(parts, axis=0).astype(f32) * score_scale
        high = q.astype(bf16)
        low = (q - high.astype(f32)).astype(bf16)
        return jnp.concatenate([high, low], axis=1)

    def limit_of(zq, yq):
        lane = lax.broadcasted_iota(jnp.int32, (8, 256), 1) % HD
        return offset + (zq * 4 + yq) * HD + lane - lax.broadcasted_iota(jnp.int32, (8, 256), 0)

    def scores(qq, limit, group, shard, start, s_ref, m):
        rows = pl.ds(start, CH)
        k = ks[2 * c + group, rows, :] if shard == 0 else kp[group, rows, :]
        kk = jnp.concatenate([k, k], axis=1)
        s = lax.dot_general(kk, qq, (((1,), (1,)), ((), ())), preferred_element_type=f32)
        s = s.reshape(CH // 8, 8, 256)
        if limit is not None:
            first_key = start + SLOTS * (c if shard == 0 else p)
            room = limit - first_key
            s = jnp.stack(
                [jnp.where(room >= 8 * i, s[i], masked_score) for i in range(CH // 8)]
            )
        s_ref[pl.ds(shard * SLOTS + start, CH), :] = s.reshape(CH, 256)
        return jnp.maximum(m, jnp.max(s, axis=0))

    def weigh(s_ref, m_now, group, shard, start, acc):
        s = s_ref[pl.ds(shard * SLOTS + start, CH), :].reshape(CH // 8, 8, 256)
        prob = jnp.exp2(s - m_now[None]).reshape(CH, 256).astype(bf16)
        cols = pl.ds(start, CH)
        vt = vs[2 * c + group, :, cols] if shard == 0 else vp[group, :, cols]
        return acc + jnp.dot(vt, prob, preferred_element_type=f32)

    steps = [(shard, start) for shard in (0, 1) for start in range(0, SLOTS, CH)]

    def tiles(new, cur, causal):
        m = jnp.full((8, 256), masked_score, f32)
        if new is not None:
            qq = queries_of(new[0], new[1], new[2])
            limit = limit_of(new[0], new[1]) if causal else None
        acc = jnp.zeros((VROWS, 256), f32)
        if cur is not None:
            m_now = tops[cur[0]]
        for shard, start in steps:
            if new is not None:
                s_ref = s1 if new[2] else s0
                m = scores(qq, limit, new[2], shard, start, s_ref, m)
            if cur is not None:
                s_ref = s1 if cur[0] else s0
                acc = weigh(s_ref, m_now, cur[0], shard, start, acc)
        if cur is not None:
            group, d, i = cur
            o_own[group, d, i] = acc[:HD].astype(bf16)
            m_own[group, d, i, 0:1, :] = m_now[0:1]
            m_own[group, d, i, 1:2, :] = acc[HD : HD + 1]
        if new is not None:
            tops[new[2]] = jnp.broadcast_to(jnp.max(m, axis=0, keepdims=True), (8, 256))

    def both(new, cur):
        @pl.when(jnp.logical_not(last_chip))
        def _():
            tiles(new, cur, False)

        @pl.when(last_chip)
        def _():
            tiles(new, cur, True)

    def tile0(d, i):
        return ahead(z, d), ahead(y, i), 0

    def tile1(d, i):
        return ahead(z, i), ahead(y, d), 1

    def sends(group, d, i):
        target = dev(ahead(z, d), y, c) if group == 0 else dev(z, ahead(y, d), c)
        return (
            remote(
                m_own.at[group, d, i], inm1.at[group, d - 1, i],
                s1ms.at[group, d - 1, i], s1mr.at[group, d - 1, i], target,
            ),
            remote(
                o_own.at[group, d, i], in1.at[group, d - 1, i],
                s1s.at[group, d - 1, i], s1r.at[group, d - 1, i], target,
            ),
        )

    first[0].wait_recv()
    for d in (1, 2, 3):
        for core in (0, 1):
            remote(
                qs.at[pl.ds(0, 2)], qg.at[z, ahead(y, 4 - d), core, pl.ds(0, 2)],
                ysend.at[d - 1, core], yrecv.at[d - 1, core], partner,
            ).wait_recv()
            remote(
                qs.at[pl.ds(0, 2)], qg.at[ahead(z, 4 - d), y, core, pl.ds(2, 2)],
                zsend.at[d - 1, core], zrecv.at[d - 1, core], partner,
            ).wait_recv()

    second = []
    for d in (3, 1, 2):
        src = qg.at[z, :, :, pl.ds(0, 2)]
        second.append(remote(src, src, fsend.at[0, d - 1], frecv.at[0, d - 1], dev(ahead(z, 4 - d), y, c)))
        src = qg.at[:, y, :, pl.ds(2, 2)]
        second.append(remote(src, src, fsend.at[1, d - 1], frecv.at[1, d - 1], dev(z, ahead(y, 4 - d), c)))
    for copy in second:
        copy.start()

    def wait_swap(b, _):
        for copy in swap_kv(b):
            copy.wait()
        return 0

    lax.fori_loop(0, BLOCKS, wait_swap, 0)
    both(tile0(0, 0), None)

    def body(u, _):
        d, i = u // 4, lax.rem(u, 4)
        both(tile1(d, i), (0, d, i))

        @pl.when(u > 4)
        def _():
            for copy in sends(1, (u - 1) // 4, lax.rem(u - 1, 4)):
                copy.start()

        @pl.when(i == 3)
        def _():
            src = qg.at[ahead(z, d + 1), :, :, pl.ds(0, 2)]
            remote(src, src, fsend.at[0, d], frecv.at[0, d], partner).wait_recv()
            src = qg.at[:, ahead(y, d + 1), :, pl.ds(2, 2)]
            remote(src, src, fsend.at[1, d], frecv.at[1, d], partner).wait_recv()

        both(tile0((u + 1) // 4, lax.rem(u + 1, 4)), (1, d, i))

        @pl.when(d > 0)
        def _():
            for copy in sends(0, d, i):
                copy.start()

        return 0

    lax.fori_loop(0, 15, body, 0)
    both(tile1(3, 3), (0, 3, 3))
    for copy in sends(1, 3, 2):
        copy.start()
    both(None, (1, 3, 3))
    for copy in sends(0, 3, 3):
        copy.start()
    for copy in sends(1, 3, 3):
        copy.start()

    for copy in first + second:
        copy.wait_send()
    for d in (1, 2, 3):
        for i in range(4):
            for group in (0, 1):
                for copy in sends(group, d, i):
                    copy.wait()

    def sum_first(i, _):
        for g in (0, 1):
            parts = [(o_own[g, 0, i], m_own[g, 0, i, 0:1, :], m_own[g, 0, i, 1:2, :])]
            for d in range(3):
                parts.append((in1[g, d, i], inm1[g, d, i, 0:1, :], inm1[g, d, i, 1:2, :]))
            numer, top, denom = merge(parts)
            mid[g, i] = numer.astype(bf16)
            midm[g, i, 0:1, :] = top
            midm[g, i, 1:2, :] = denom
        return 0

    lax.fori_loop(0, 4, sum_first, 0)
    third = []
    for i in (2, 1, 3):
        for g in (0, 1):
            target = dev(z, ahead(y, i), c) if g == 0 else dev(ahead(z, i), y, c)
            third.append(remote(midm.at[g, i], inm2.at[g, i - 1], s2ms.at[g, i - 1], s2mr.at[g, i - 1], target))
            third.append(remote(mid.at[g, i], in2.at[g, i - 1], s2s.at[g, i - 1], s2r.at[g, i - 1], target))
    for copy in third:
        copy.start()
    for copy in third:
        copy.wait()
    for g in (0, 1):
        parts = [(mid[g, 0], midm[g, 0, 0:1, :], midm[g, 0, 1:2, :])]
        for i in range(3):
            parts.append((in2[g, i], inm2[g, i, 0:1, :], inm2[g, i, 1:2, :]))
        numer, _, denom = merge(parts)
        done = numer / denom
        for h in (0, 1):
            rows = done[:, h * HD : (h + 1) * HD].T.astype(bf16)
            cols = slice((g * 2 + h) * HD, (g * 2 + h + 1) * HD)
            half[0, :, cols] = rows[:ROWS]
            half[1, :, cols] = rows[ROWS:]

    swap = remote(half.at[p], att.at[c], as_, ar, partner)
    swap.start()
    load_w.wait()
    swap.wait()
    lhs = jnp.concatenate(
        [jnp.where(c == 0, half[0], att[0]), jnp.where(c == 0, att[1], half[1])], axis=1
    )
    fourth = []
    for d in (2, 1, 3, 0):
        target = ahead(head, d)
        cols = pl.ds(pl.multiple_of(target * COLS, HD), COLS)
        block = jnp.dot(lhs, w[:, cols], preferred_element_type=f32)
        if d:
            part[d - 1] = block.astype(bf16)
            copy = remote(part.at[d - 1], inx.at[d - 1], xs.at[d - 1], xr.at[d - 1], (seq, target))
            copy.start()
            fourth.append(copy)
        else:
            total = block
    for copy in fourth:
        copy.wait()
    out_ref[...] = total + ((inx[0].astype(f32) + inx[1].astype(f32)) + inx[2].astype(f32))


def shards(queries, keys, values, kv_len, causal_offset, out_weight):
    dma = pltpu.SemaphoreType.DMA
    hbm = pl.BlockSpec(memory_space=pl.ANY)
    smem = pl.BlockSpec(memory_space=pltpu.SMEM)

    def vmem(*shape, dtype=bf16):
        return pltpu.VMEM(shape, dtype)

    return pl.pallas_call(
        kernel,
        out_shape=jax.ShapeDtypeStruct((ROWS, COLS), f32),
        in_specs=[smem, smem, hbm, hbm, hbm, hbm],
        out_specs=pl.BlockSpec(memory_space=pltpu.VMEM),
        scratch_shapes=[
            vmem(ROWS * 8, HD),
            vmem(SLOTS * 4, HD),
            vmem(SLOTS * 4, HD),
            vmem(1024, 4608),
            vmem(BLOCK * 4, HD, dtype=f32),
            vmem(8, ROWS, HD),
            vmem(4, SLOTS, HD),
            vmem(4, VROWS, SLOTS),
            vmem(2, SLOTS, HD),
            vmem(2, VROWS, SLOTS),
            vmem(4, 4, 2, 4, ROWS, HD),
            vmem(2 * SLOTS, 256, dtype=f32),
            vmem(2 * SLOTS, 256, dtype=f32),
            vmem(2, 8, 256, dtype=f32),
            vmem(2, 4, 4, HD, 256),
            vmem(2, 4, 4, 2, 256, dtype=f32),
            vmem(2, 3, 4, HD, 256),
            vmem(2, 3, 4, 2, 256, dtype=f32),
            vmem(2, 4, HD, 256),
            vmem(2, 4, 2, 256, dtype=f32),
            vmem(2, 3, HD, 256),
            vmem(2, 3, 2, 256, dtype=f32),
            vmem(2, ROWS, 512),
            vmem(2, ROWS, 512),
            vmem(3, ROWS, COLS),
            vmem(3, ROWS, COLS),
            dma((2,)), dma((BLOCKS,)), dma((BLOCKS,)),
            dma, dma,
            dma((3, 2)), dma((3, 2)), dma((3, 2)), dma((3, 2)),
            dma((2, 3)), dma((2, 3)),
            dma((BLOCKS,)), dma((BLOCKS,)), dma((BLOCKS,)), dma((BLOCKS,)),
            dma((2, 3, 4)), dma((2, 3, 4)), dma((2, 3, 4)), dma((2, 3, 4)),
            dma((2, 3)), dma((2, 3)), dma((2, 3)), dma((2, 3)),
            dma, dma,
            dma((3,)), dma((3,)),
        ],
        compiler_params=pltpu.CompilerParams(
            collective_id=0, has_side_effects=True, vmem_limit_bytes=60 * 2**20
        ),
        name="attend",
    )(
        kv_len,
        causal_offset,
        queries.reshape(ROWS * 8, HD),
        keys.reshape(SLOTS * 4, HD),
        values.reshape(SLOTS * 4, HD),
        out_weight,
    )


def solution(mesh):
    placed = (
        P("seq", "head", None),
        P("seq", "head", None),
        P("seq", "head", None),
        P("seq"),
        P(),
        P("head", None),
    )
    return jax.shard_map(
        shards, mesh=mesh, in_specs=placed, out_specs=P("seq", "head"), check_vma=False
    )
```

time: 479 us -> 78.4 us (0.16); the launches traced: 472 us -> 78.3 us
  matrix products: 149 us -> 0 us
  waiting for transfers between devices: 129 us -> 0 us
  Pallas kernels: 0 us -> 75.3 us
  other arithmetic: 72.3 us -> 0 us
  local copies, waits for them, and re-layouts: 69.8 us -> 1.69 us
  starting transfers between devices: 20.3 us -> 0 us
  blocking collectives: 14.3 us -> 0 us
  between operations: 13.6 us -> 1.31 us
    dot_general x9 -> x0, matrix products: 149 us -> none  [the longest x4 78 us: step(): jnp.einsum('qgrk,kgd->qgrd', weights.astype(jnp.bfloat16), value_block, p...]
    all_to_all x3 -> x0, waiting for transfers between devices: 76.1 us -> none  [the longest x1 76 us: shards(): lax.all_to_all(numer[None], 'seq', split_axis=1, concat_axis=0, tiled=True)]
    pallas_call x0 -> x1, Pallas kernels: none -> 75.3 us  [shards(): pl.pallas_call(kernel, out_shape=jax.ShapeDtypeStruct((ROWS, COLS), f32),...]
    reduce_sum x7 -> x0, other arithmetic: 60.5 us -> none  [the longest x4 57.1 us: step(): denom = denom * factor + jnp.sum(weights, axis=-1)]
    all_gather x1 -> x0, waiting for transfers between devices: 52.1 us -> none  [shards(): query_all = lax.all_gather(queries, 'seq', axis=0, tiled=True)]
    unnamed x7 -> x1, local copies, waits for them, and re-layouts: 23.6 us -> 1.69 us
    all_to_all x3 -> x0, starting transfers between devices: 20.3 us -> none  [the longest x1 7.44 us: shards(): lax.all_to_all(numer[None], 'seq', split_axis=1, concat_axis=0, tiled=True)]
    while x7 -> x0, local copies, waits for them, and re-layouts: 15.4 us -> none  [the longest x3 15.4 us: shards(): lax.scan(step, init, jnp.arange(block_count, dtype=jnp.int32))]
  transfers between devices with their start and end apart: 4 -> 0, of which waited for: 2 -> 0; matrix products, arithmetic and copies ran while one was open for 10% -> 0% of each run, Pallas kernels for 0% -> 0%
where the time goes in v2:
time: 78.4 us; the launch traced here: 78.3 us
  Pallas kernels  75.3 us (96%)
  local copies, waits for them, and re-layouts  1.69 us (2%)
  between operations  1.31 us (2%)
    pallas_call x1, Pallas kernels, shards(): pl.pallas_call(kernel, out_shape=jax.ShapeDtypeStruct((ROWS, COLS), f32),...  75.3 us
    unnamed x1, local copies, waits for them, and re-layouts  1.69 us

profile of v2, /device:TPU:1, one launch (start us, length us, event | category | flops | bytes accessed | tf_op | source)
XLA Modules:
  0.0 78.3 jit_solution(2470479867382417001)
XLA Ops:
  1.3 75.3 %attend.1 = f32[64,1152]{1,0:T(8,128)} custom-call(s32[1]{0:T(128)S(6)} %copy.8.len_ref, s32[1]{0:T(128)S(6)} %copy.9.off_ref, bf16[512,128]{1,0:T(8,128)(2,1)} %bitcast.5, bf16[8192,128]{1,0:T(8,128)(2,1)} %bitcast.3, bf16[8192,128]{1,0:T(8,128)(2,1)} %bitcast.4, bf16[1024,4608]{1,0:T(8,128)(2,1)} %w_hbm.1), custom_call_target="tpu_custom_call" | custom-call | tf_op jit(solution)/shard_map/attend/pallas_call | solution.py:391
  76.6 1.7 %copy.10 = f32[64,1152]{1,0:T(8,128)} copy(f32[64,1152]{1,0:T(8,128)} %attend.1) | data formatting | bytes 589824

commit v3 on v2

--- a/solution.py
+++ b/solution.py
@@ -49,10 +49,10 @@
 
 def kernel(
     len_ref, off_ref, q_hbm, k_hbm, v_hbm, w_hbm, out_ref,
-    q_raw, k_raw, v_raw, w, wide, qs, ks, vs, kp, vp, qg, s0, s1, tops,
-    o_own, m_own, in1, inm1, mid, midm, in2, inm2, half, att, part, inx,
+    q_raw, k_raw, v_raw, w_vmem, wide, qs, ks, vs, kp, vp, qg, s0, s1, tops,
+    o_own, m_own, in1, inm1, mid, midm, in2, inm2, lhs, part, total, inx,
     lsem, kl, vl, psend, precv, ysend, yrecv, zsend, zrecv, fsend, frecv,
-    ksend, krecv, vsend, vrecv, s1s, s1r, s1ms, s1mr, s2s, s2r, s2ms, s2mr, as_, ar, xs, xr,
+    ksend, krecv, vsend, vrecv, s1s, s1r, s1ms, s1mr, s2s, s2r, s2ms, s2mr, xs, xr,
 ):
     seq = lax.axis_index("seq")
     head = lax.axis_index("head")
@@ -68,7 +68,7 @@
     partner = dev(z, y, p)
 
     load_q = pltpu.make_async_copy(q_hbm, q_raw, lsem.at[0])
-    load_w = pltpu.make_async_copy(w_hbm, w, lsem.at[1])
+    load_w = pltpu.make_async_copy(w_hbm, w_vmem, lsem.at[1])
 
     def load_kv(b):
         rows = pl.ds(pl.multiple_of(b * BLOCK * 4, BLOCK * 4), BLOCK * 4)
@@ -81,7 +81,6 @@
     for b in range(BLOCKS):
         for copy in load_kv(b):
             copy.start()
-    load_w.start()
 
     peers = [partner]
     for d in (1, 2, 3):
@@ -160,20 +159,29 @@
     lax.fori_loop(0, BLOCKS // 2, start_swap, 0)
     lax.fori_loop(BLOCKS // 2, BLOCKS, prepare, 0)
     lax.fori_loop(BLOCKS // 2, BLOCKS, start_swap, 0)
+    load_w.start()
 
     last_chip = (z == 3) & (y == 3)
     offset = off_ref[0] - 30 * SLOTS
 
-    def queries_of(zq, yq, group):
-        parts = [qg[zq, yq, core, group * 2 + h] for h in (0, 1) for core in (0, 1)]
+    def chips(group, d, j):
+        if group == 0:
+            return [(ahead(z, d), ahead(y, 2 * j + e)) for e in (0, 1)]
+        return [(ahead(z, 2 * j + e), ahead(y, d)) for e in (0, 1)]
+
+    def queries_of(group, w, d, j):
+        parts = [qg[zq, yq, w, group * 2 + h] for zq, yq in chips(group, d, j) for h in (0, 1)]
         q = jnp.concatenate(parts, axis=0).astype(f32) * score_scale
         high = q.astype(bf16)
         low = (q - high.astype(f32)).astype(bf16)
         return jnp.concatenate([high, low], axis=1)
 
-    def limit_of(zq, yq):
-        lane = lax.broadcasted_iota(jnp.int32, (8, 256), 1) % HD
-        return offset + (zq * 4 + yq) * HD + lane - lax.broadcasted_iota(jnp.int32, (8, 256), 0)
+    def limit_of(group, w, d, j):
+        lane = lax.broadcasted_iota(jnp.int32, (8, 256), 1)
+        (za, ya), (zb, yb) = chips(group, d, j)
+        chip = jnp.where(lane < HD, za * 4 + ya, zb * 4 + yb)
+        row = chip * HD + w * ROWS + lane % ROWS
+        return offset + row - lax.broadcasted_iota(jnp.int32, (8, 256), 0)
 
     def scores(qq, limit, group, shard, start, s_ref, m):
         rows = pl.ds(start, CH)
@@ -202,25 +210,25 @@
     def tiles(new, cur, causal):
         m = jnp.full((8, 256), masked_score, f32)
         if new is not None:
-            qq = queries_of(new[0], new[1], new[2])
-            limit = limit_of(new[0], new[1]) if causal else None
+            qq = queries_of(*new)
+            limit = limit_of(*new) if causal else None
         acc = jnp.zeros((VROWS, 256), f32)
         if cur is not None:
             m_now = tops[cur[0]]
         for shard, start in steps:
             if new is not None:
-                s_ref = s1 if new[2] else s0
-                m = scores(qq, limit, new[2], shard, start, s_ref, m)
+                s_ref = s1 if new[0] else s0
+                m = scores(qq, limit, new[0], shard, start, s_ref, m)
             if cur is not None:
                 s_ref = s1 if cur[0] else s0
                 acc = weigh(s_ref, m_now, cur[0], shard, start, acc)
         if cur is not None:
-            group, d, i = cur
-            o_own[group, d, i] = acc[:HD].astype(bf16)
-            m_own[group, d, i, 0:1, :] = m_now[0:1]
-            m_own[group, d, i, 1:2, :] = acc[HD : HD + 1]
+            group, w, d, j = cur
+            o_own[group, w, d, j] = acc[:HD].astype(bf16)
+            m_own[group, w, d, j, 0:1, :] = m_now[0:1]
+            m_own[group, w, d, j, 1:2, :] = acc[HD : HD + 1]
         if new is not None:
-            tops[new[2]] = jnp.broadcast_to(jnp.max(m, axis=0, keepdims=True), (8, 256))
+            tops[new[0]] = jnp.broadcast_to(jnp.max(m, axis=0, keepdims=True), (8, 256))
 
     def both(new, cur):
         @pl.when(jnp.logical_not(last_chip))
@@ -231,23 +239,129 @@
         def _():
             tiles(new, cur, True)
 
-    def tile0(d, i):
-        return ahead(z, d), ahead(y, i), 0
-
-    def tile1(d, i):
-        return ahead(z, i), ahead(y, d), 1
-
-    def sends(group, d, i):
+    def step(u):
+        w = u // 8
+        k = lax.rem(lax.rem(u, 8) // 2 + w, 4)
+        return w, lax.rem(k * (k + 1) // 2, 4), lax.rem(u, 2)
+
+    def sends(group, w, d, j):
         target = dev(ahead(z, d), y, c) if group == 0 else dev(z, ahead(y, d), c)
+        slot = (group, w, d - 1, j)
+        return (
+            remote(m_own.at[group, w, d, j], inm1.at[slot], s1ms.at[slot], s1mr.at[slot], target),
+            remote(o_own.at[group, w, d, j], in1.at[slot], s1s.at[slot], s1r.at[slot], target),
+        )
+
+    def send_tile(group, u):
+        w, d, j = step(u)
+
+        @pl.when(d > 0)
+        def _():
+            for copy in sends(group, w, d, j):
+                copy.start()
+
+    def passes(group, w, i):
+        if i == 0:
+            target = partner
+        else:
+            target = dev(z, ahead(y, i), w) if group == 0 else dev(ahead(z, i), y, w)
         return (
             remote(
-                m_own.at[group, d, i], inm1.at[group, d - 1, i],
-                s1ms.at[group, d - 1, i], s1mr.at[group, d - 1, i], target,
+                midm.at[group, w, i], inm2.at[c, group, i],
+                s2ms.at[group, w, i], s2mr.at[c, group, i], target,
             ),
             remote(
-                o_own.at[group, d, i], in1.at[group, d - 1, i],
-                s1s.at[group, d - 1, i], s1r.at[group, d - 1, i], target,
+                mid.at[group, w, i], in2.at[c, group, i],
+                s2s.at[group, w, i], s2r.at[c, group, i], target,
             ),
+        )
+
+    def sum_first(group, w, j):
+        for d in (1, 2, 3):
+            for copy in sends(group, w, d, j):
+                copy.wait_recv()
+        parts = [
+            (o_own[group, w, 0, j], m_own[group, w, 0, j, 0:1, :], m_own[group, w, 0, j, 1:2, :])
+        ]
+        for d in range(3):
+            parts.append(
+                (in1[group, w, d, j], inm1[group, w, d, j, 0:1, :], inm1[group, w, d, j, 1:2, :])
+            )
+        numer, top, denom = merge(parts)
+        for e in (0, 1):
+            i = 2 * j + e
+            lanes = slice(e * HD, (e + 1) * HD)
+            mid[group, w, i] = numer[:, lanes].astype(bf16)
+            midm[group, w, i, 0:1, :] = top[:, lanes]
+            midm[group, w, i, 1:2, :] = denom[:, lanes]
+        for e in (1, 0):
+            i = 2 * j + e
+            if i:
+                for copy in passes(group, w, i):
+                    copy.start()
+            else:
+
+                @pl.when(c != w)
+                def _():
+                    for copy in passes(group, w, 0):
+                        copy.start()
+
+                @pl.when(c == w)
+                def _():
+                    in2[c, group, 0] = mid[group, w, 0]
+                    inm2[c, group, 0] = midm[group, w, 0]
+
+    def exchange(d):
+        return remote(
+            part.at[d - 1], inx.at[d - 1], xs.at[d - 1], xr.at[d - 1], (seq, ahead(head, d))
+        )
+
+    def project(w):
+        for group in (0, 1):
+            for source in (0, 1):
+                for i in range(4):
+                    if i or source != w:
+                        slot = (source, group, i)
+                        remote(
+                            midm.at[group, w, i], inm2.at[slot],
+                            s2ms.at[group, w, i], s2mr.at[slot], partner,
+                        ).wait_recv()
+                        remote(
+                            mid.at[group, w, i], in2.at[slot],
+                            s2s.at[group, w, i], s2r.at[slot], partner,
+                        ).wait_recv()
+        for source in (0, 1):
+            for group in (0, 1):
+                parts = [
+                    (
+                        in2[source, group, i],
+                        inm2[source, group, i, 0:1, :],
+                        inm2[source, group, i, 1:2, :],
+                    )
+                    for i in range(4)
+                ]
+                numer, _, denom = merge(parts)
+                rows = (numer / denom).T.astype(bf16)
+                first_col = (source * 2 + group) * 2 * HD
+                for h in (0, 1):
+                    cols = slice(first_col + h * HD, first_col + (h + 1) * HD)
+                    lhs[:, cols] = rows[h * ROWS : (h + 1) * ROWS]
+        load_w.wait()
+        left = lhs[...]
+        for d in (2, 1, 3, 0):
+            cols = pl.ds(pl.multiple_of(ahead(head, d) * COLS, HD), COLS)
+            block = jnp.dot(left, w_vmem[:, cols], preferred_element_type=f32)
+            if d:
+                part[d - 1] = block.astype(bf16)
+                exchange(d).start()
+            else:
+                total[...] = block
+
+    def finish():
+        for d in (1, 2, 3):
+            exchange(d).wait()
+        out_ref[...] = total[...] + (
+            (inx[0].astype(f32) + inx[1].astype(f32)) + inx[2].astype(f32)
         )
 
     first[0].wait_recv()
@@ -262,12 +376,17 @@
                 zsend.at[d - 1, core], zrecv.at[d - 1, core], partner,
             ).wait_recv()
 
-    second = []
-    for d in (3, 1, 2):
-        src = qg.at[z, :, :, pl.ds(0, 2)]
-        second.append(remote(src, src, fsend.at[0, d - 1], frecv.at[0, d - 1], dev(ahead(z, 4 - d), y, c)))
-        src = qg.at[:, y, :, pl.ds(2, 2)]
-        second.append(remote(src, src, fsend.at[1, d - 1], frecv.at[1, d - 1], dev(z, ahead(y, 4 - d), c)))
+    def forward(group, w, d, back):
+        if group == 0:
+            src = qg.at[ahead(z, d) if back else z, :, w, pl.ds(0, 2)]
+            target = dev(ahead(z, 4 - d), y, c)
+        else:
+            src = qg.at[:, ahead(y, d) if back else y, w, pl.ds(2, 2)]
+            target = dev(z, ahead(y, 4 - d), c)
+        slot = (group, w, d - 1)
+        return remote(src, src, fsend.at[slot], frecv.at[slot], target)
+
+    second = [forward(g, w, d, False) for w in (0, 1) for d in (1, 3, 2) for g in (0, 1)]
     for copy in second:
         copy.start()
 
@@ -277,107 +396,70 @@
         return 0
 
     lax.fori_loop(0, BLOCKS, wait_swap, 0)
-    both(tile0(0, 0), None)
+    both((0, *step(0)), None)
 
     def body(u, _):
-        d, i = u // 4, lax.rem(u, 4)
-        both(tile1(d, i), (0, d, i))
-
-        @pl.when(u > 4)
-        def _():
-            for copy in sends(1, (u - 1) // 4, lax.rem(u - 1, 4)):
-                copy.start()
-
-        @pl.when(i == 3)
-        def _():
-            src = qg.at[ahead(z, d + 1), :, :, pl.ds(0, 2)]
-            remote(src, src, fsend.at[0, d], frecv.at[0, d], partner).wait_recv()
-            src = qg.at[:, ahead(y, d + 1), :, pl.ds(2, 2)]
-            remote(src, src, fsend.at[1, d], frecv.at[1, d], partner).wait_recv()
-
-        both(tile0((u + 1) // 4, lax.rem(u + 1, 4)), (1, d, i))
-
-        @pl.when(d > 0)
-        def _():
-            for copy in sends(0, d, i):
-                copy.start()
+        both((1, *step(u)), (0, *step(u)))
+
+        @pl.when(u > 0)
+        def _():
+            send_tile(1, u - 1)
+
+        w, d, j = step(u + 1)
+
+        @pl.when((j == 0) & (d > 0))
+        def _():
+            for group in (0, 1):
+                forward(group, w, d, True).wait_recv()
+
+        both((0, w, d, j), (1, *step(u)))
+        send_tile(0, u)
+
+        @pl.when(u == 10)
+        def _():
+            for j in (0, 1):
+                for group in (0, 1):
+                    sum_first(group, 0, j)
+
+        @pl.when((u == 12) & (c == 0))
+        def _():
+            project(0)
+
+        @pl.when(u == 14)
+        def _():
+            sum_first(0, 1, 0)
+            sum_first(1, 1, 0)
 
         return 0
 
     lax.fori_loop(0, 15, body, 0)
-    both(tile1(3, 3), (0, 3, 3))
-    for copy in sends(1, 3, 2):
-        copy.start()
-    both(None, (1, 3, 3))
-    for copy in sends(0, 3, 3):
-        copy.start()
-    for copy in sends(1, 3, 3):
-        copy.start()
+    both((1, 1, 0, 1), (0, 1, 0, 1))
+    sum_first(0, 1, 1)
+    both(None, (1, 1, 0, 1))
+    sum_first(1, 1, 1)
+
+    @pl.when(c == 1)
+    def _():
+        project(1)
 
     for copy in first + second:
         copy.wait_send()
-    for d in (1, 2, 3):
-        for i in range(4):
-            for group in (0, 1):
-                for copy in sends(group, d, i):
-                    copy.wait()
-
-    def sum_first(i, _):
-        for g in (0, 1):
-            parts = [(o_own[g, 0, i], m_own[g, 0, i, 0:1, :], m_own[g, 0, i, 1:2, :])]
-            for d in range(3):
-                parts.append((in1[g, d, i], inm1[g, d, i, 0:1, :], inm1[g, d, i, 1:2, :]))
-            numer, top, denom = merge(parts)
-            mid[g, i] = numer.astype(bf16)
-            midm[g, i, 0:1, :] = top
-            midm[g, i, 1:2, :] = denom
-        return 0
-
-    lax.fori_loop(0, 4, sum_first, 0)
-    third = []
-    for i in (2, 1, 3):
-        for g in (0, 1):
-            target = dev(z, ahead(y, i), c) if g == 0 else dev(ahead(z, i), y, c)
-            third.append(remote(midm.at[g, i], inm2.at[g, i - 1], s2ms.at[g, i - 1], s2mr.at[g, i - 1], target))
-            third.append(remote(mid.at[g, i], in2.at[g, i - 1], s2s.at[g, i - 1], s2r.at[g, i - 1], target))
-    for copy in third:
-        copy.start()
-    for copy in third:
-        copy.wait()
-    for g in (0, 1):
-        parts = [(mid[g, 0], midm[g, 0, 0:1, :], midm[g, 0, 1:2, :])]
-        for i in range(3):
-            parts.append((in2[g, i], inm2[g, i, 0:1, :], inm2[g, i, 1:2, :]))
-        numer, _, denom = merge(parts)
-        done = numer / denom
-        for h in (0, 1):
-            rows = done[:, h * HD : (h + 1) * HD].T.astype(bf16)
-            cols = slice((g * 2 + h) * HD, (g * 2 + h + 1) * HD)
-            half[0, :, cols] = rows[:ROWS]
-            half[1, :, cols] = rows[ROWS:]
-
-    swap = remote(half.at[p], att.at[c], as_, ar, partner)
-    swap.start()
-    load_w.wait()
-    swap.wait()
-    lhs = jnp.concatenate(
-        [jnp.where(c == 0, half[0], att[0]), jnp.where(c == 0, att[1], half[1])], axis=1
-    )
-    fourth = []
-    for d in (2, 1, 3, 0):
-        target = ahead(head, d)
-        cols = pl.ds(pl.multiple_of(target * COLS, HD), COLS)
-        block = jnp.dot(lhs, w[:, cols], preferred_element_type=f32)
-        if d:
-            part[d - 1] = block.astype(bf16)
-            copy = remote(part.at[d - 1], inx.at[d - 1], xs.at[d - 1], xr.at[d - 1], (seq, target))
-            copy.start()
-            fourth.append(copy)
-        else:
-            total = block
-    for copy in fourth:
-        copy.wait()
-    out_ref[...] = total + ((inx[0].astype(f32) + inx[1].astype(f32)) + inx[2].astype(f32))
+    for group in (0, 1):
+        for w in (0, 1):
+            for j in (0, 1):
+                for d in (1, 2, 3):
+                    for copy in sends(group, w, d, j):
+                        copy.wait_send()
+            for i in (1, 2, 3):
+                for copy in passes(group, w, i):
+                    copy.wait_send()
+
+            @pl.when(c != w)
+            def _():
+                for copy in passes(group, w, 0):
+                    copy.wait_send()
+
+    finish()
 
 
 def shards(queries, keys, values, kv_len, causal_offset, out_weight):
@@ -408,26 +490,25 @@
             vmem(2 * SLOTS, 256, dtype=f32),
             vmem(2 * SLOTS, 256, dtype=f32),
             vmem(2, 8, 256, dtype=f32),
-            vmem(2, 4, 4, HD, 256),
-            vmem(2, 4, 4, 2, 256, dtype=f32),
-            vmem(2, 3, 4, HD, 256),
-            vmem(2, 3, 4, 2, 256, dtype=f32),
-            vmem(2, 4, HD, 256),
-            vmem(2, 4, 2, 256, dtype=f32),
-            vmem(2, 3, HD, 256),
-            vmem(2, 3, 2, 256, dtype=f32),
-            vmem(2, ROWS, 512),
-            vmem(2, ROWS, 512),
+            vmem(2, 2, 4, 2, HD, 256),
+            vmem(2, 2, 4, 2, 2, 256, dtype=f32),
+            vmem(2, 2, 3, 2, HD, 256),
+            vmem(2, 2, 3, 2, 2, 256, dtype=f32),
+            vmem(2, 2, 4, HD, HD),
+            vmem(2, 2, 4, 2, HD, dtype=f32),
+            vmem(2, 2, 4, HD, HD),
+            vmem(2, 2, 4, 2, HD, dtype=f32),
+            vmem(ROWS, 1024),
             vmem(3, ROWS, COLS),
+            vmem(ROWS, COLS, dtype=f32),
             vmem(3, ROWS, COLS),
             dma((2,)), dma((BLOCKS,)), dma((BLOCKS,)),
             dma, dma,
             dma((3, 2)), dma((3, 2)), dma((3, 2)), dma((3, 2)),
-            dma((2, 3)), dma((2, 3)),
+            dma((2, 2, 3)), dma((2, 2, 3)),
             dma((BLOCKS,)), dma((BLOCKS,)), dma((BLOCKS,)), dma((BLOCKS,)),
-            dma((2, 3, 4)), dma((2, 3, 4)), dma((2, 3, 4)), dma((2, 3, 4)),
-            dma((2, 3)), dma((2, 3)), dma((2, 3)), dma((2, 3)),
-            dma, dma,
+            dma((2, 2, 3, 2)), dma((2, 2, 3, 2)), dma((2, 2, 3, 2)), dma((2, 2, 3, 2)),
+            dma((2, 2, 4)), dma((2, 2, 4)), dma((2, 2, 4)), dma((2, 2, 4)),
             dma((3,)), dma((3,)),
         ],
         compiler_params=pltpu.CompilerParams(

time: 78.4 us -> 76.8 us (0.980); the launches traced: 78.3 us -> 75.7 us
  Pallas kernels: 75.3 us -> 72.7 us
    pallas_call x1, Pallas kernels: 75.3 us -> 72.7 us  [shards(): pl.pallas_call(kernel, out_shape=jax.ShapeDtypeStruct((ROWS, COLS), f32),...]
where the time goes in v3:
time: 76.8 us; the launch traced here: 75.7 us
  Pallas kernels  72.7 us (95%)
  local copies, waits for them, and re-layouts  1.69 us (2%)
  between operations  1.31 us (2%)
    pallas_call x1, Pallas kernels, shards(): pl.pallas_call(kernel, out_shape=jax.ShapeDtypeStruct((ROWS, COLS), f32),...  72.7 us
    unnamed x1, local copies, waits for them, and re-layouts  1.69 us

profile of v3, /device:TPU:1, one launch (start us, length us, event | category | flops | bytes accessed | tf_op | source)
XLA Modules:
  0.0 75.7 jit_solution(2324597662479297343)
XLA Ops:
  1.3 72.7 %attend.1 = f32[64,1152]{1,0:T(8,128)} custom-call(s32[1]{0:T(128)S(6)} %copy.8.len_ref, s32[1]{0:T(128)S(6)} %copy.9.off_ref, bf16[512,128]{1,0:T(8,128)(2,1)} %bitcast.5, bf16[8192,128]{1,0:T(8,128)(2,1)} %bitcast.3, bf16[8192,128]{1,0:T(8,128)(2,1)} %bitcast.4, bf16[1024,4608]{1,0:T(8,128)(2,1)} %w_hbm.1), custom_call_target="tpu_custom_call" | custom-call | tf_op jit(solution)/shard_map/attend/pallas_call | solution.py:473
  74.0 1.7 %copy.10 = f32[64,1152]{1,0:T(8,128)} copy(f32[64,1152]{1,0:T(8,128)} %attend.1) | data formatting | bytes 589824

commit v4 on v3

--- a/solution.py
+++ b/solution.py
@@ -16,7 +16,6 @@
 ROWS = 64
 SLOTS = 2048
 VROWS = 144
-CH = 256
 COLS = 1152
 BLOCK = 256
 BLOCKS = SLOTS // BLOCK
@@ -49,7 +48,7 @@
 
 def kernel(
     len_ref, off_ref, q_hbm, k_hbm, v_hbm, w_hbm, out_ref,
-    q_raw, k_raw, v_raw, w_vmem, wide, qs, ks, vs, kp, vp, qg, s0, s1, tops,
+    q_raw, k_raw, v_raw, w_vmem, wide, qs, ks, vs, kp, vp, qg, sa0, sa1, sb0, sb1, tops,
     o_own, m_own, in1, inm1, mid, midm, in2, inm2, lhs, part, total, inx,
     lsem, kl, vl, psend, precv, ysend, yrecv, zsend, zrecv, fsend, frecv,
     ksend, krecv, vsend, vrecv, s1s, s1r, s1ms, s1mr, s2s, s2r, s2ms, s2mr, xs, xr,
@@ -117,20 +116,24 @@
         ones = jnp.where((col < length) & (row == 0), 1.0, 0.0).astype(bf16)
         for h in range(4):
             one = wide[pl.ds(h, BLOCK, stride=4), :]
-            vs[h, 0:HD, slots] = jnp.where(filled, one, 0.0).T.astype(bf16)
-            vs[h, HD:VROWS, slots] = ones
+            one = jnp.where(filled, one, 0.0).T.astype(bf16)
+            for e in range(BLOCK // HD):
+                lanes = slice(e * HD, (e + 1) * HD)
+                vs[h, b * (BLOCK // HD) + e, 0:HD, :] = one[:, lanes]
+                vs[h, b * (BLOCK // HD) + e, HD:VROWS, :] = ones[:, lanes]
         return 0
 
     def swap_kv(b):
         slots = pl.ds(pl.multiple_of(b * BLOCK, BLOCK), BLOCK)
+        parts = pl.ds(b * (BLOCK // HD), BLOCK // HD)
         return (
             remote(ks.at[pl.ds(2 * p, 2), slots], kp.at[:, slots], ksend.at[b], krecv.at[b], partner),
             remote(
-                vs.at[pl.ds(2 * p, 2), :, slots], vp.at[:, :, slots], vsend.at[b], vrecv.at[b], partner
+                vs.at[pl.ds(2 * p, 2), parts], vp.at[:, parts], vsend.at[b], vrecv.at[b], partner
             ),
         )
 
-    lax.fori_loop(0, BLOCKS // 2, prepare, 0)
+    lax.fori_loop(0, 2, prepare, 0)
     pl.semaphore_wait(barrier, len(peers))
 
     first = [remote(qs.at[pl.ds(4 * p, 4)], qg.at[z, y, c], psend, precv, partner)]
@@ -148,17 +151,35 @@
                     zsend.at[d - 1, core], zrecv.at[d - 1, c], dev(ahead(z, d), y, core),
                 )
             )
-    for copy in first:
-        copy.start()
-
-    def start_swap(b, _):
+
+    @pl.when(c == 0)
+    def _():
+        for copy in first:
+            copy.start()
+
+    for b in (0, 1):
         for copy in swap_kv(b):
             copy.start()
+
+    def prepare_and_swap(b, _):
+        prepare(b, 0)
+
+        @pl.when(b > 2)
+        def _():
+            for copy in swap_kv(b - 1):
+                copy.start()
+
         return 0
 
-    lax.fori_loop(0, BLOCKS // 2, start_swap, 0)
-    lax.fori_loop(BLOCKS // 2, BLOCKS, prepare, 0)
-    lax.fori_loop(BLOCKS // 2, BLOCKS, start_swap, 0)
+    lax.fori_loop(2, BLOCKS, prepare_and_swap, 0)
+
+    @pl.when(c == 1)
+    def _():
+        for copy in first:
+            copy.start()
+
+    for copy in swap_kv(BLOCKS - 1):
+        copy.start()
     load_w.start()
 
     last_chip = (z == 3) & (y == 3)
@@ -183,61 +204,61 @@
         row = chip * HD + w * ROWS + lane % ROWS
         return offset + row - lax.broadcasted_iota(jnp.int32, (8, 256), 0)
 
-    def scores(qq, limit, group, shard, start, s_ref, m):
-        rows = pl.ds(start, CH)
-        k = ks[2 * c + group, rows, :] if shard == 0 else kp[group, rows, :]
+    def scores(qq, limit, group, shard, s_ref, m):
+        k = ks[2 * c + group] if shard == 0 else kp[group]
         kk = jnp.concatenate([k, k], axis=1)
         s = lax.dot_general(kk, qq, (((1,), (1,)), ((), ())), preferred_element_type=f32)
-        s = s.reshape(CH // 8, 8, 256)
+        s = s.reshape(SLOTS // 8, 8, 256)
         if limit is not None:
-            first_key = start + SLOTS * (c if shard == 0 else p)
-            room = limit - first_key
+            room = limit - SLOTS * (c if shard == 0 else p)
             s = jnp.stack(
-                [jnp.where(room >= 8 * i, s[i], masked_score) for i in range(CH // 8)]
+                [jnp.where(room >= 8 * i, s[i], masked_score) for i in range(SLOTS // 8)]
             )
-        s_ref[pl.ds(shard * SLOTS + start, CH), :] = s.reshape(CH, 256)
+        s_ref[pl.ds(shard * SLOTS, SLOTS), :] = s.reshape(SLOTS, 256)
         return jnp.maximum(m, jnp.max(s, axis=0))
 
-    def weigh(s_ref, m_now, group, shard, start, acc):
-        s = s_ref[pl.ds(shard * SLOTS + start, CH), :].reshape(CH // 8, 8, 256)
-        prob = jnp.exp2(s - m_now[None]).reshape(CH, 256).astype(bf16)
-        cols = pl.ds(start, CH)
-        vt = vs[2 * c + group, :, cols] if shard == 0 else vp[group, :, cols]
-        return acc + jnp.dot(vt, prob, preferred_element_type=f32)
-
-    steps = [(shard, start) for shard in (0, 1) for start in range(0, SLOTS, CH)]
-
-    def tiles(new, cur, causal):
-        m = jnp.full((8, 256), masked_score, f32)
-        if new is not None:
-            qq = queries_of(*new)
-            limit = limit_of(*new) if causal else None
-        acc = jnp.zeros((VROWS, 256), f32)
-        if cur is not None:
-            m_now = tops[cur[0]]
-        for shard, start in steps:
+    def weigh(s_ref, m_now, group, shard, acc):
+        s = s_ref[pl.ds(shard * SLOTS, SLOTS), :].reshape(SLOTS // 8, 8, 256)
+        prob = jnp.exp2(s - m_now[None]).reshape(SLOTS, 256).astype(bf16)
+        parts = [
+            vs[2 * c + group, e] if shard == 0 else vp[group, e] for e in range(SLOTS // HD)
+        ]
+        return acc + jnp.dot(jnp.concatenate(parts, axis=1), prob, preferred_element_type=f32)
+
+    score_refs = ((sa0, sa1), (sb0, sb1))
+
+    def tiles(new, cur, side, causal):
+        for group in (0, 1):
+            m = jnp.full((8, 256), masked_score, f32)
             if new is not None:
-                s_ref = s1 if new[0] else s0
-                m = scores(qq, limit, new[0], shard, start, s_ref, m)
+                qq = queries_of(group, *new)
+                limit = limit_of(group, *new) if causal else None
             if cur is not None:
-                s_ref = s1 if cur[0] else s0
-                acc = weigh(s_ref, m_now, cur[0], shard, start, acc)
-        if cur is not None:
-            group, w, d, j = cur
-            o_own[group, w, d, j] = acc[:HD].astype(bf16)
-            m_own[group, w, d, j, 0:1, :] = m_now[0:1]
-            m_own[group, w, d, j, 1:2, :] = acc[HD : HD + 1]
-        if new is not None:
-            tops[new[0]] = jnp.broadcast_to(jnp.max(m, axis=0, keepdims=True), (8, 256))
-
-    def both(new, cur):
-        @pl.when(jnp.logical_not(last_chip))
-        def _():
-            tiles(new, cur, False)
-
-        @pl.when(last_chip)
-        def _():
-            tiles(new, cur, True)
+                m_now = tops[side, group]
+            acc = jnp.zeros((VROWS, 256), f32)
+            for shard in (0, 1):
+                if new is not None:
+                    m = scores(qq, limit, group, shard, score_refs[1 - side][group], m)
+                if cur is not None:
+                    acc = weigh(score_refs[side][group], m_now, group, shard, acc)
+            if cur is not None:
+                w, d, j = cur
+                o_own[group, w, d, j] = acc[:HD].astype(bf16)
+                m_own[group, w, d, j, 0:1, :] = m_now[0:1]
+                m_own[group, w, d, j, 1:2, :] = acc[HD : HD + 1]
+            if new is not None:
+                tops[1 - side, group] = jnp.broadcast_to(
+                    jnp.max(m, axis=0, keepdims=True), (8, 256)
+                )
+
+    def both(new, cur, side, when=True):
+        @pl.when(jnp.logical_not(last_chip) & when)
+        def _():
+            tiles(new, cur, side, False)
+
+        @pl.when(last_chip & when)
+        def _():
+            tiles(new, cur, side, True)
 
     def step(u):
         w = u // 8
@@ -364,9 +385,12 @@
             (inx[0].astype(f32) + inx[1].astype(f32)) + inx[2].astype(f32)
         )
 
-    first[0].wait_recv()
-    for d in (1, 2, 3):
-        for core in (0, 1):
+    def wait_first(core):
+        @pl.when(c != core)
+        def _():
+            first[0].wait_recv()
+
+        for d in (1, 2, 3):
             remote(
                 qs.at[pl.ds(0, 2)], qg.at[z, ahead(y, 4 - d), core, pl.ds(0, 2)],
                 ysend.at[d - 1, core], yrecv.at[d - 1, core], partner,
@@ -375,6 +399,8 @@
                 qs.at[pl.ds(0, 2)], qg.at[ahead(z, 4 - d), y, core, pl.ds(2, 2)],
                 zsend.at[d - 1, core], zrecv.at[d - 1, core], partner,
             ).wait_recv()
+
+    wait_first(0)
 
     def forward(group, w, d, back):
         if group == 0:
@@ -386,9 +412,14 @@
         slot = (group, w, d - 1)
         return remote(src, src, fsend.at[slot], frecv.at[slot], target)
 
-    second = [forward(g, w, d, False) for w in (0, 1) for d in (1, 3, 2) for g in (0, 1)]
-    for copy in second:
-        copy.start()
+    second = {(w, d): [forward(g, w, d, False) for g in (0, 1)] for w in (0, 1) for d in (1, 3, 2)}
+
+    def start_forward(w, *ds):
+        for d in ds:
+            for copy in second[w, d]:
+                copy.start()
+
+    start_forward(0, 1, 3)
 
     def wait_swap(b, _):
         for copy in swap_kv(b):
@@ -396,54 +427,73 @@
         return 0
 
     lax.fori_loop(0, BLOCKS, wait_swap, 0)
-    both((0, *step(0)), None)
-
-    def body(u, _):
-        both((1, *step(u)), (0, *step(u)))
-
-        @pl.when(u > 0)
-        def _():
-            send_tile(1, u - 1)
-
-        w, d, j = step(u + 1)
-
-        @pl.when((j == 0) & (d > 0))
+    both(step(0), None, 1)
+
+    def after(u):
+        send_tile(0, u)
+        send_tile(1, u)
+
+        @pl.when(u == 0)
+        def _():
+            start_forward(0, 2)
+
+        @pl.when(u == 2)
+        def _():
+            wait_first(1)
+            start_forward(1, 1, 3)
+
+        @pl.when(u == 4)
+        def _():
+            start_forward(1, 2)
+
+        w, d, j = step(u + 2)
+
+        @pl.when((j == 0) & (d > 0) & (u < 14))
         def _():
             for group in (0, 1):
                 forward(group, w, d, True).wait_recv()
 
-        both((0, w, d, j), (1, *step(u)))
-        send_tile(0, u)
-
-        @pl.when(u == 10)
+        @pl.when(u == 9)
         def _():
             for j in (0, 1):
                 for group in (0, 1):
                     sum_first(group, 0, j)
 
-        @pl.when((u == 12) & (c == 0))
+        @pl.when((u == 11) & (c == 0))
         def _():
             project(0)
 
         @pl.when(u == 14)
         def _():
-            sum_first(0, 1, 0)
-            sum_first(1, 1, 0)
+            for group in (0, 1):
+                sum_first(group, 1, 0)
+
+    def body(v, _):
+        u = 2 * v
+        both(step(u + 1), step(u), 0)
+        after(u)
+        both(step(u + 2), step(u + 1), 1, u < 14)
+
+        @pl.when(u < 14)
+        def _():
+            after(u + 1)
 
         return 0
 
-    lax.fori_loop(0, 15, body, 0)
-    both((1, 1, 0, 1), (0, 1, 0, 1))
-    sum_first(0, 1, 1)
-    both(None, (1, 1, 0, 1))
-    sum_first(1, 1, 1)
+    lax.fori_loop(0, 8, body, 0)
+    both(None, step(15), 1)
+    for group in (0, 1):
+        sum_first(group, 1, 1)
 
     @pl.when(c == 1)
     def _():
         project(1)
 
-    for copy in first + second:
+    for copy in first:
         copy.wait_send()
+    for copies in second.values():
+        for copy in copies:
+            copy.wait_send()
     for group in (0, 1):
         for w in (0, 1):
             for j in (0, 1):
@@ -483,13 +533,15 @@
             vmem(BLOCK * 4, HD, dtype=f32),
             vmem(8, ROWS, HD),
             vmem(4, SLOTS, HD),
-            vmem(4, VROWS, SLOTS),
+            vmem(4, SLOTS // HD, VROWS, HD),
             vmem(2, SLOTS, HD),
-            vmem(2, VROWS, SLOTS),
+            vmem(2, SLOTS // HD, VROWS, HD),
             vmem(4, 4, 2, 4, ROWS, HD),
             vmem(2 * SLOTS, 256, dtype=f32),
             vmem(2 * SLOTS, 256, dtype=f32),
-            vmem(2, 8, 256, dtype=f32),
+            vmem(2 * SLOTS, 256, dtype=f32),
+            vmem(2 * SLOTS, 256, dtype=f32),
+            vmem(2, 2, 8, 256, dtype=f32),
             vmem(2, 2, 4, 2, HD, 256),
             vmem(2, 2, 4, 2, 2, 256, dtype=f32),
             vmem(2, 2, 3, 2, HD, 256),

time: 76.8 us -> 70.4 us (0.917); the launches traced: 75.7 us -> 70.2 us
  Pallas kernels: 72.7 us -> 67.2 us
    pallas_call x1, Pallas kernels: 72.7 us -> 67.2 us  [shards(): pl.pallas_call(kernel, out_shape=jax.ShapeDtypeStruct((ROWS, COLS), f32),...]
where the time goes in v4:
time: 70.4 us; the launch traced here: 70.2 us
  Pallas kernels  67.2 us (95%)
  local copies, waits for them, and re-layouts  1.69 us (2%)
  between operations  1.31 us (2%)
    pallas_call x1, Pallas kernels, shards(): pl.pallas_call(kernel, out_shape=jax.ShapeDtypeStruct((ROWS, COLS), f32),...  67.2 us
    unnamed x1, local copies, waits for them, and re-layouts  1.69 us

profile of v4, /device:TPU:1, one launch (start us, length us, event | category | flops | bytes accessed | tf_op | source)
XLA Modules:
  0.0 70.2 jit_solution(5389817959297625650)
XLA Ops:
  1.3 67.2 %attend.1 = f32[64,1152]{1,0:T(8,128)} custom-call(s32[1]{0:T(128)S(6)} %copy.8.len_ref, s32[1]{0:T(128)S(6)} %copy.9.off_ref, bf16[512,128]{1,0:T(8,128)(2,1)} %bitcast.5, bf16[8192,128]{1,0:T(8,128)(2,1)} %bitcast.3, bf16[8192,128]{1,0:T(8,128)(2,1)} %bitcast.4, bf16[1024,4608]{1,0:T(8,128)(2,1)} %w_hbm.1), custom_call_target="tpu_custom_call" | custom-call | tf_op jit(solution)/shard_map/attend/pallas_call | solution.py:523
  68.5 1.7 %copy.10 = f32[64,1152]{1,0:T(8,128)} copy(f32[64,1152]{1,0:T(8,128)} %attend.1) | data formatting | bytes 589824

commit v5 on v4

--- a/solution.py
+++ b/solution.py
@@ -133,7 +133,6 @@
             ),
         )
 
-    lax.fori_loop(0, 2, prepare, 0)
     pl.semaphore_wait(barrier, len(peers))
 
     first = [remote(qs.at[pl.ds(4 * p, 4)], qg.at[z, y, c], psend, precv, partner)]
@@ -157,21 +156,17 @@
         for copy in first:
             copy.start()
 
-    for b in (0, 1):
-        for copy in swap_kv(b):
-            copy.start()
-
     def prepare_and_swap(b, _):
         prepare(b, 0)
 
-        @pl.when(b > 2)
+        @pl.when(b > 0)
         def _():
             for copy in swap_kv(b - 1):
                 copy.start()
 
         return 0
 
-    lax.fori_loop(2, BLOCKS, prepare_and_swap, 0)
+    lax.fori_loop(0, BLOCKS, prepare_and_swap, 0)
 
     @pl.when(c == 1)
     def _():
@@ -262,8 +257,9 @@
 
     def step(u):
         w = u // 8
-        k = lax.rem(lax.rem(u, 8) // 2 + w, 4)
-        return w, lax.rem(k * (k + 1) // 2, 4), lax.rem(u, 2)
+        k = lax.rem(u, 8) // 2
+        d = (1 - w) * lax.rem(k * (k + 1) // 2, 4) + w * (3 - k)
+        return w, d, lax.rem(u, 2)
 
     def sends(group, w, d, j):
         target = dev(ahead(z, d), y, c) if group == 0 else dev(z, ahead(y, d), c)
@@ -426,8 +422,25 @@
             copy.wait()
         return 0
 
-    lax.fori_loop(0, BLOCKS, wait_swap, 0)
-    both(step(0), None, 1)
+    def open_with(shard, causal):
+        for group in (0, 1):
+            qq = queries_of(group, *step(0))
+            limit = limit_of(group, *step(0)) if causal else None
+            m = tops[0, group] if shard else jnp.full((8, 256), masked_score, f32)
+            m = scores(qq, limit, group, shard, score_refs[0][group], m)
+            tops[0, group] = jnp.broadcast_to(jnp.max(m, axis=0, keepdims=True), (8, 256))
+
+    for shard in (0, 1):
+        if shard:
+            lax.fori_loop(0, BLOCKS, wait_swap, 0)
+
+        @pl.when(jnp.logical_not(last_chip))
+        def _():
+            open_with(shard, False)
+
+        @pl.when(last_chip)
+        def _():
+            open_with(shard, True)
 
     def after(u):
         send_tile(0, u)
@@ -440,11 +453,11 @@
         @pl.when(u == 2)
         def _():
             wait_first(1)
-            start_forward(1, 1, 3)
+            start_forward(1, 3, 2)
 
         @pl.when(u == 4)
         def _():
-            start_forward(1, 2)
+            start_forward(1, 1)
 
         w, d, j = step(u + 2)
 
@@ -458,10 +471,6 @@
             for j in (0, 1):
                 for group in (0, 1):
                     sum_first(group, 0, j)
-
-        @pl.when((u == 11) & (c == 0))
-        def _():
-            project(0)
 
         @pl.when(u == 14)
         def _():
@@ -484,6 +493,10 @@
     both(None, step(15), 1)
     for group in (0, 1):
         sum_first(group, 1, 1)
+
+    @pl.when(c == 0)
+    def _():
+        project(0)
 
     @pl.when(c == 1)
     def _():

time: 70.4 us -> 68.8 us (0.977)
  Pallas kernels: 67.2 us -> 65.6 us
    pallas_call x1, Pallas kernels: 67.2 us -> 65.6 us  [shards(): pl.pallas_call(kernel, out_shape=jax.ShapeDtypeStruct((ROWS, COLS), f32),...]
where the time goes in v5:
time: 68.8 us; the launch traced here: 68.6 us
  Pallas kernels  65.6 us (95%)
  local copies, waits for them, and re-layouts  1.69 us (2%)
  between operations  1.31 us (2%)
    pallas_call x1, Pallas kernels, shards(): pl.pallas_call(kernel, out_shape=jax.ShapeDtypeStruct((ROWS, COLS), f32),...  65.6 us
    unnamed x1, local copies, waits for them, and re-layouts  1.69 us

profile of v5, /device:TPU:1, one launch (start us, length us, event | category | flops | bytes accessed | tf_op | source)
XLA Modules:
  0.0 68.6 jit_solution(865307469397166429)
XLA Ops:
  1.3 65.6 %attend.1 = f32[64,1152]{1,0:T(8,128)} custom-call(s32[1]{0:T(128)S(6)} %copy.8.len_ref, s32[1]{0:T(128)S(6)} %copy.9.off_ref, bf16[512,128]{1,0:T(8,128)(2,1)} %bitcast.5, bf16[8192,128]{1,0:T(8,128)(2,1)} %bitcast.3, bf16[8192,128]{1,0:T(8,128)(2,1)} %bitcast.4, bf16[1024,4608]{1,0:T(8,128)(2,1)} %w_hbm.1), custom_call_target="tpu_custom_call" | custom-call | tf_op jit(solution)/shard_map/attend/pallas_call | solution.py:536
  67.0 1.7 %copy.10 = f32[64,1152]{1,0:T(8,128)} copy(f32[64,1152]{1,0:T(8,128)} %attend.1) | data formatting | bytes 589824

commit v6 on v5

--- a/solution.py
+++ b/solution.py
@@ -258,7 +258,8 @@
     def step(u):
         w = u // 8
         k = lax.rem(u, 8) // 2
-        d = (1 - w) * lax.rem(k * (k + 1) // 2, 4) + w * (3 - k)
+        k = lax.rem(k + w, 4)
+        d = lax.rem(k * (k + 1) // 2, 4)
         return w, d, lax.rem(u, 2)
 
     def sends(group, w, d, j):
@@ -381,11 +382,12 @@
             (inx[0].astype(f32) + inx[1].astype(f32)) + inx[2].astype(f32)
         )
 
+    def wait_partner(core):
+        @pl.when(c != core)
+        def _():
+            first[0].wait_recv()
+
     def wait_first(core):
-        @pl.when(c != core)
-        def _():
-            first[0].wait_recv()
-
         for d in (1, 2, 3):
             remote(
                 qs.at[pl.ds(0, 2)], qg.at[z, ahead(y, 4 - d), core, pl.ds(0, 2)],
@@ -396,26 +398,26 @@
                 zsend.at[d - 1, core], zrecv.at[d - 1, core], partner,
             ).wait_recv()
 
-    wait_first(0)
-
-    def forward(group, w, d, back):
+    def forward(group, w, d, e, back):
         if group == 0:
-            src = qg.at[ahead(z, d) if back else z, :, w, pl.ds(0, 2)]
+            src = qg.at[ahead(z, d) if back else z, ahead(y, e), w, pl.ds(0, 2)]
             target = dev(ahead(z, 4 - d), y, c)
         else:
-            src = qg.at[:, ahead(y, d) if back else y, w, pl.ds(2, 2)]
+            src = qg.at[ahead(z, e), ahead(y, d) if back else y, w, pl.ds(2, 2)]
             target = dev(z, ahead(y, 4 - d), c)
-        slot = (group, w, d - 1)
+        slot = (group, w, d - 1, e)
         return remote(src, src, fsend.at[slot], frecv.at[slot], target)
 
-    second = {(w, d): [forward(g, w, d, False) for g in (0, 1)] for w in (0, 1) for d in (1, 3, 2)}
-
-    def start_forward(w, *ds):
-        for d in ds:
-            for copy in second[w, d]:
-                copy.start()
-
-    start_forward(0, 1, 3)
+    def start_forward(w, ds, es):
+        for e in es:
+            for d in ds:
+                for group in (0, 1):
+                    forward(group, w, d, e, False).start()
+
+    wait_partner(0)
+    start_forward(0, (1, 3), (0,))
+    wait_first(0)
+    start_forward(0, (1, 3), (1, 2, 3))
 
     def wait_swap(b, _):
         for copy in swap_kv(b):
@@ -448,23 +450,25 @@
 
         @pl.when(u == 0)
         def _():
-            start_forward(0, 2)
+            start_forward(0, (2,), (0, 1, 2, 3))
 
         @pl.when(u == 2)
         def _():
+            wait_partner(1)
             wait_first(1)
-            start_forward(1, 3, 2)
+            start_forward(1, (1, 3), (0, 1, 2, 3))
 
         @pl.when(u == 4)
         def _():
-            start_forward(1, 1)
+            start_forward(1, (2,), (0, 1, 2, 3))
 
         w, d, j = step(u + 2)
 
-        @pl.when((j == 0) & (d > 0) & (u < 14))
+        @pl.when((d > 0) & (u < 14))
         def _():
             for group in (0, 1):
-                forward(group, w, d, True).wait_recv()
+                for e in (0, 1):
+                    forward(group, w, d, 2 * j + e, True).wait_recv()
 
         @pl.when(u == 9)
         def _():
@@ -504,9 +508,11 @@
 
     for copy in first:
         copy.wait_send()
-    for copies in second.values():
-        for copy in copies:
-            copy.wait_send()
+    for w in (0, 1):
+        for d in (1, 2, 3):
+            for e in range(4):
+                for group in (0, 1):
+                    forward(group, w, d, e, False).wait_send()
     for group in (0, 1):
         for w in (0, 1):
             for j in (0, 1):
@@ -570,7 +576,7 @@
             dma((2,)), dma((BLOCKS,)), dma((BLOCKS,)),
             dma, dma,
             dma((3, 2)), dma((3, 2)), dma((3, 2)), dma((3, 2)),
-            dma((2, 2, 3)), dma((2, 2, 3)),
+            dma((2, 2, 3, 4)), dma((2, 2, 3, 4)),
             dma((BLOCKS,)), dma((BLOCKS,)), dma((BLOCKS,)), dma((BLOCKS,)),
             dma((2, 2, 3, 2)), dma((2, 2, 3, 2)), dma((2, 2, 3, 2)), dma((2, 2, 3, 2)),
             dma((2, 2, 4)), dma((2, 2, 4)), dma((2, 2, 4)), dma((2, 2, 4)),

time: 68.8 us -> 66.5 us (0.967)
  Pallas kernels: 65.6 us -> 63.4 us
    pallas_call x1, Pallas kernels: 65.6 us -> 63.4 us  [shards(): pl.pallas_call(kernel, out_shape=jax.ShapeDtypeStruct((ROWS, COLS), f32),...]
where the time goes in v6:
time: 66.5 us; the launch traced here: 66.4 us
  Pallas kernels  63.4 us (95%)
  local copies, waits for them, and re-layouts  1.69 us (3%)
  between operations  1.31 us (2%)
    pallas_call x1, Pallas kernels, shards(): pl.pallas_call(kernel, out_shape=jax.ShapeDtypeStruct((ROWS, COLS), f32),...  63.4 us
    unnamed x1, local copies, waits for them, and re-layouts  1.69 us

profile of v6, /device:TPU:1, one launch (start us, length us, event | category | flops | bytes accessed | tf_op | source)
XLA Modules:
  0.0 66.4 jit_solution(13134442478824670883)
XLA Ops:
  1.3 63.4 %attend.1 = f32[64,1152]{1,0:T(8,128)} custom-call(s32[1]{0:T(128)S(6)} %copy.8.len_ref, s32[1]{0:T(128)S(6)} %copy.9.off_ref, bf16[512,128]{1,0:T(8,128)(2,1)} %bitcast.5, bf16[8192,128]{1,0:T(8,128)(2,1)} %bitcast.3, bf16[8192,128]{1,0:T(8,128)(2,1)} %bitcast.4, bf16[1024,4608]{1,0:T(8,128)(2,1)} %w_hbm.1), custom_call_target="tpu_custom_call" | custom-call | tf_op jit(solution)/shard_map/attend/pallas_call | solution.py:542
  64.7 1.7 %copy.10 = f32[64,1152]{1,0:T(8,128)} copy(f32[64,1152]{1,0:T(8,128)} %attend.1) | data formatting | bytes 589824

commit v7 on v6

--- a/solution.py
+++ b/solution.py
@@ -533,7 +533,7 @@
 
 def shards(queries, keys, values, kv_len, causal_offset, out_weight):
     dma = pltpu.SemaphoreType.DMA
-    hbm = pl.BlockSpec(memory_space=pl.ANY)
+    hbm = pl.BlockSpec(memory_space=pltpu.HBM)
     smem = pl.BlockSpec(memory_space=pltpu.SMEM)
 
     def vmem(*shape, dtype=bf16):
@@ -583,7 +583,7 @@
             dma((3,)), dma((3,)),
         ],
         compiler_params=pltpu.CompilerParams(
-            collective_id=0, has_side_effects=True, vmem_limit_bytes=60 * 2**20
+            collective_id=0, has_side_effects=True, vmem_limit_bytes=53 * 2**20
         ),
         name="attend",
     )(

time: 66.5 us -> 65.3 us (0.982)
  Pallas kernels: 63.4 us -> 62.2 us
    pallas_call x1, Pallas kernels: 63.4 us -> 62.2 us  [shards(): pl.pallas_call(kernel, out_shape=jax.ShapeDtypeStruct((ROWS, COLS), f32),...]
    unnamed x1 -> x3, local copies, waits for them, and re-layouts: 1.69 us -> 1.61 us
where the time goes in v7:
time: 65.3 us; the launch traced here: 65.1 us
  Pallas kernels  62.2 us (95%)
  local copies, waits for them, and re-layouts  1.61 us (2%)
  between operations  1.31 us (2%)
    pallas_call x1, Pallas kernels, shards(): pl.pallas_call(kernel, out_shape=jax.ShapeDtypeStruct((ROWS, COLS), f32),...  62.2 us
    unnamed x3, local copies, waits for them, and re-layouts  1.61 us

profile of v7, /device:TPU:1, one launch (start us, length us, event | category | flops | bytes accessed | tf_op | source)
XLA Modules:
  0.0 65.1 jit_solution(7747212945344590313)
XLA Ops:
  1.3 0.0 copy-start
  1.3 0.9 %copy-done = bf16[64,8,128]{2,1,0:T(8,128)(2,1)S(1)} copy-done((bf16[64,8,128]{2,1,0:T(8,128)(2,1)S(1)}, bf16[64,8,128]{2,1,0:T(8,128)(2,1)}, u32[]{:S(2)}) %copy-start) | copy-done | bytes 131096
  2.2 62.2 %attend.1 = f32[64,1152]{1,0:T(8,128)S(1)} custom-call(s32[1]{0:T(128)S(6)} %copy.8.len_ref, s32[1]{0:T(128)S(6)} %copy.9.off_ref, bf16[512,128]{1,0:T(8,128)(2,1)S(1)} %bitcast.3, bf16[8192,128]{1,0:T(8,128)(2,1)} %bitcast.4, bf16[8192,128]{1,0:T(8,128)(2,1)} %bitcast.5, bf16[1024,4608]{1,0:T(8,128)(2,1)} %w_hbm.1), custom_call_target="tpu_custom_call" | custom-call | tf_op jit(solution)/shard_map/attend/pallas_call | solution.py:542
  64.4 0.7 %copy.10 = f32[64,1152]{1,0:T(8,128)} copy(f32[64,1152]{1,0:T(8,128)S(1)} %attend.1) | data formatting | bytes 589824
Async XLA Ops:
  1.3 0.9 %copy-start = (bf16[64,8,128]{2,1,0:T(8,128)(2,1)S(1)}, bf16[64,8,128]{2,1,0:T(8,128)(2,1)}, u32[]{:S(2)}) copy-start(bf16[64,8,128]{2,1,0:T(8,128)(2,1)} %param.6) | copy-start | bytes 393220

commit v8 on v7

--- a/solution.py
+++ b/solution.py
@@ -452,13 +452,13 @@
         def _():
             start_forward(0, (2,), (0, 1, 2, 3))
 
-        @pl.when(u == 2)
+        @pl.when(u == 1)
         def _():
             wait_partner(1)
             wait_first(1)
             start_forward(1, (1, 3), (0, 1, 2, 3))
 
-        @pl.when(u == 4)
+        @pl.when(u == 3)
         def _():
             start_forward(1, (2,), (0, 1, 2, 3))
 
@@ -470,7 +470,7 @@
                 for e in (0, 1):
                     forward(group, w, d, 2 * j + e, True).wait_recv()
 
-        @pl.when(u == 9)
+        @pl.when(u == 11)
         def _():
             for j in (0, 1):
                 for group in (0, 1):

time: 65.3 us -> 65.3 us (level)
  no operation moved by 1% of the time
where the time goes in v8:
time: 65.3 us; the launch traced here: 65.1 us
  Pallas kernels  62.2 us (95%)
  local copies, waits for them, and re-layouts  1.61 us (2%)
  between operations  1.31 us (2%)
    pallas_call x1, Pallas kernels, shards(): pl.pallas_call(kernel, out_shape=jax.ShapeDtypeStruct((ROWS, COLS), f32),...  62.2 us
    unnamed x3, local copies, waits for them, and re-layouts  1.61 us

profile of v8, /device:TPU:1, one launch (start us, length us, event | category | flops | bytes accessed | tf_op | source)
XLA Modules:
  0.0 65.1 jit_solution(10027092039461188168)
XLA Ops:
  1.3 0.0 copy-start
  1.3 0.9 %copy-done = bf16[64,8,128]{2,1,0:T(8,128)(2,1)S(1)} copy-done((bf16[64,8,128]{2,1,0:T(8,128)(2,1)S(1)}, bf16[64,8,128]{2,1,0:T(8,128)(2,1)}, u32[]{:S(2)}) %copy-start) | copy-done | bytes 131096
  2.2 62.2 %attend.1 = f32[64,1152]{1,0:T(8,128)S(1)} custom-call(s32[1]{0:T(128)S(6)} %copy.8.len_ref, s32[1]{0:T(128)S(6)} %copy.9.off_ref, bf16[512,128]{1,0:T(8,128)(2,1)S(1)} %bitcast.3, bf16[8192,128]{1,0:T(8,128)(2,1)} %bitcast.4, bf16[8192,128]{1,0:T(8,128)(2,1)} %bitcast.5, bf16[1024,4608]{1,0:T(8,128)(2,1)} %w_hbm.1), custom_call_target="tpu_custom_call" | custom-call | tf_op jit(solution)/shard_map/attend/pallas_call | solution.py:542
  64.4 0.7 %copy.10 = f32[64,1152]{1,0:T(8,128)} copy(f32[64,1152]{1,0:T(8,128)S(1)} %attend.1) | data formatting | bytes 589824
Async XLA Ops:
  1.3 0.9 %copy-start = (bf16[64,8,128]{2,1,0:T(8,128)(2,1)S(1)}, bf16[64,8,128]{2,1,0:T(8,128)(2,1)}, u32[]{:S(2)}) copy-start(bf16[64,8,128]{2,1,0:T(8,128)(2,1)} %param.6) | copy-start | bytes 393220
